TPU v7x, 32 devices: a whole 2x2x4 slice. The times are simulated.
32 devices in a mesh: rep: 4 (over y, x), fsdp: 8 (over z, core).
Axes of the slice: x: 2, y: 2, z: 4, core: 2. Of those that a mesh axis runs over, the one named last changes fastest.
Arguments:
- home_tokens: bfloat16 [4, 8, 1024, 1024], P('rep', None, 'fsdp'), may hold values from -6 to 6
- home_encoder: bfloat16 [4, 8, 512, 1024], P('rep', None, 'fsdp'), may hold values from -6 to 6
- out_grad: bfloat16 [4, 8, 1024, 1024], P('rep', 'fsdp'), may hold values from -6 to 6
- lengths: int32 [4, 8], P('rep'), may hold values from 1 to 1024, 6144 in all within a row
- enc_lengths: int32 [4, 8], P('rep'), may hold values from 1 to 512, 3072 in all within a row
- seq_order: int32 [4, 8], P('rep'), may hold values from 0 to 7, each once within a row
- attn_master: float32 [8, 1024, 1024], P(None, 'fsdp'), may hold values from -2 to 2
- ffin_master: float32 [2, 1024, 2816], P(None, 'fsdp'), may hold values from -0.1875 to 0.1875
- ffout_master: float32 [1024, 2816], P('fsdp'), may hold values from -0.109375 to 0.109375
- gain_master: float32 [3, 1024], P(None, 'fsdp'), may hold values from 0.5 to 1.5
- decays: float32 [4], replicated, may hold values from 0.4 to 0.6
- attn_left: float32 [8, 16, 16, 4096], P(None, 'fsdp'), may hold values from -0.15 to 2, as said below
- attn_right: float32 [8, 16, 16, 4096], P(None, 'fsdp'), may hold values from -0.15 to 2, as said below
- attn_left_root: float32 [8, 16, 16, 4096], P(None, 'fsdp'), may hold values from -0.15 to 2, as said below
- attn_right_root: float32 [8, 16, 16, 4096], P(None, 'fsdp'), may hold values from -0.15 to 2, as said below
- ffin_left: float32 [2, 16, 44, 4096], P(None, 'fsdp'), may hold values from -0.15 to 2, as said below
- ffin_right: float32 [2, 16, 44, 4096], P(None, 'fsdp'), may hold values from -0.15 to 2, as said below
- ffin_left_root: float32 [2, 16, 44, 4096], P(None, 'fsdp'), may hold values from -0.15 to 2, as said below
- ffin_right_root: float32 [2, 16, 44, 4096], P(None, 'fsdp'), may hold values from -0.15 to 2, as said below
- ffout_left: float32 [16, 44, 4096], P('fsdp'), may hold values from -0.15 to 2, as said below
- ffout_right: float32 [16, 44, 4096], P('fsdp'), may hold values from -0.15 to 2, as said below
- ffout_left_root: float32 [16, 44, 4096], P('fsdp'), may hold values from -0.15 to 2, as said below
- ffout_right_root: float32 [16, 44, 4096], P('fsdp'), may hold values from -0.15 to 2, as said below
- gain_stats: float32 [3, 1024], P(None, 'fsdp'), may hold values from 0.5 to 2
Outputs:
- out_tokens: bfloat16 [4, 8, 1024, 1024], P('rep', 'fsdp')
- token_grad: bfloat16 [4, 8, 1024, 1024], P('rep', None, 'fsdp')
- encoder_grad: bfloat16 [4, 8, 512, 1024], P('rep', None, 'fsdp')
- attn_grad: float32 [8, 1024, 1024], P(None, 'fsdp')
- ffin_grad: float32 [2, 1024, 2816], P(None, 'fsdp')
- ffout_grad: float32 [1024, 2816], P('fsdp')
- gain_grad: float32 [3, 1024], P(None, 'fsdp')
- attn_update: float32 [8, 1024, 1024], P(None, 'fsdp')
- ffin_update: float32 [2, 1024, 2816], P(None, 'fsdp')
- ffout_update: float32 [1024, 2816], P('fsdp')
- gain_update: float32 [3, 1024], P(None, 'fsdp')
- attn_left_new: float32 [8, 16, 16, 4096], P(None, 'fsdp')
- attn_right_new: float32 [8, 16, 16, 4096], P(None, 'fsdp')
- ffin_left_new: float32 [2, 16, 44, 4096], P(None, 'fsdp')
- ffin_right_new: float32 [2, 16, 44, 4096], P(None, 'fsdp')
- ffout_left_new: float32 [16, 44, 4096], P('fsdp')
- ffout_right_new: float32 [16, 44, 4096], P('fsdp')
- gain_stats_new: float32 [3, 1024], P(None, 'fsdp')
Inputs may be any that keep to these rules, and one draw needn't show every extreme that they name: Row r lists the decoder lengths of the 8 sequences of group r. `enc_lengths`: row r lists the encoder lengths of the 8 sequences of group r. `seq_order`: each row is a permutation of the group's sequences. `attn_left`: each row of the last dimension is a symmetric block. `attn_right`: each row of the last dimension is a symmetric block. `attn_left_root`: each row of the last dimension is a symmetric block. `attn_right_root`: each row of the last dimension is a symmetric block. `ffin_left`: each row of the last dimension is a symmetric block. `ffin_right`: each row of the last dimension is a symmetric block. `ffin_left_root`: each row of the last dimension is a symmetric block. `ffin_right_root`: each row of the last dimension is a symmetric block. `ffout_left`: each row of the last dimension is a symmetric block. `ffout_right`: each row of the last dimension is a symmetric block. `ffout_left_root`: each row of the last dimension is a symmetric block. `ffout_right_root`: each row of the last dimension is a symmetric block.
All inputs are finite; a program needn't handle non-finite values.
Results may differ from a plain program's by a relative error of at most 0.029.
The roundings to bfloat16 on the way count: a program that leaves them out, or rounds other values in their place, can miss the bound.
Values may be sent and summed in bfloat16 or wider, within the bound.
A program may use at most 448 MiB of HBM per device.

v0:
```python
import jax
import jax.numpy as jnp
from jax import lax
from jax.sharding import PartitionSpec as P

D = 1024
HEADS = 16
HEAD = 64
TILE = 64
SEQ_LEN = 1024
ENC_LEN = 512
QROWS = 512


highest = lax.Precision.HIGHEST
norm_eps = 1e-06
stat_eps = 1e-06
masked_score = -1e30


def rms_scale(inputs, gain_row):
    return (
        inputs * lax.rsqrt(jnp.mean(inputs * inputs, axis=-1, keepdims=True) + norm_eps) * gain_row
    )


def gelu_tanh(inputs):
    return (
        0.5
        * inputs
        * (1.0 + jnp.tanh(0.7978845608 * (inputs + 0.044715 * inputs * inputs * inputs)))
    )


def gated_unit(gate_part, up_part):
    return gelu_tanh(gate_part) * up_part


def lookup(table_row, chosen):
    slot_ids = jnp.arange(table_row.shape[0], dtype=jnp.int32)
    return jnp.sum(jnp.where(chosen[:, None] == slot_ids[None, :], table_row[None, :], 0), axis=1)


def block_mask(first_row, row_count, key_count, key_limit, causal):
    key_pos = jnp.arange(key_count, dtype=jnp.int32)
    allowed = key_pos[None, :] < key_limit
    if causal:
        query_pos = first_row + jnp.arange(row_count, dtype=jnp.int32)
        allowed = allowed & (key_pos[None, :] <= query_pos[:, None])
    return allowed[None]


def block_scores(query_block, key_rows, first_row, key_limit, causal):
    scores = jnp.einsum("qhd,khd->hqk", query_block, key_rows, preferred_element_type=jnp.float32)
    allowed = block_mask(first_row, query_block.shape[0], key_rows.shape[0], key_limit, causal)
    return jnp.where(allowed, scores, masked_score)


def attend_forward(queries, key_rows, value_rows, key_limit, query_limit, causal):
    head_count = queries.shape[1]
    blended_parts = []
    total_parts = []
    for first_row in range(0, queries.shape[0], QROWS):
        query_block = queries[first_row : first_row + QROWS]

        def compute(query_block, first_row=first_row):
            scores = block_scores(query_block, key_rows, first_row, key_limit, causal)
            row_max = jnp.max(scores, axis=-1, keepdims=True)
            exp_scores = jnp.exp(scores - row_max)
            row_total = jnp.sum(exp_scores, axis=-1, keepdims=True)
            soft_weights = (exp_scores / row_total).astype(jnp.bfloat16)
            blended = jnp.einsum(
                "hqk,khd->qhd", soft_weights, value_rows, preferred_element_type=jnp.float32
            )
            return (blended.astype(jnp.bfloat16), (row_max + jnp.log(row_total))[..., 0])

        def skipped(query_block):
            return (
                jnp.zeros(query_block.shape, jnp.bfloat16),
                jnp.zeros((head_count, query_block.shape[0]), jnp.float32),
            )

        blended, log_total = lax.cond(first_row < query_limit, compute, skipped, query_block)
        blended_parts.append(blended)
        total_parts.append(log_total)
    return (jnp.concatenate(blended_parts, 0), jnp.concatenate(total_parts, 1))


def attend_backward(
    queries, key_rows, value_rows, log_totals, grad_rows, key_limit, query_limit, causal
):
    query_parts = []
    grad_keys = jnp.zeros(key_rows.shape, jnp.float32)
    grad_values = jnp.zeros(value_rows.shape, jnp.float32)
    for first_row in range(0, queries.shape[0], QROWS):
        operands = (
            queries[first_row : first_row + QROWS],
            log_totals[:, first_row : first_row + QROWS],
            grad_rows[first_row : first_row + QROWS],
            grad_keys,
            grad_values,
        )

        def compute(operands, first_row=first_row):
            query_block, total_block, grad_block, keys_sum, values_sum = operands
            scores = block_scores(query_block, key_rows, first_row, key_limit, causal)
            soft_weights = jnp.exp(scores - total_block[..., None])
            grad_soft = jnp.einsum(
                "qhd,khd->hqk", grad_block, value_rows, preferred_element_type=jnp.float32
            )
            values_sum = values_sum + jnp.einsum(
                "hqk,qhd->khd",
                soft_weights.astype(jnp.bfloat16),
                grad_block,
                preferred_element_type=jnp.float32,
            )
            row_inner = jnp.sum(grad_soft * soft_weights, axis=-1, keepdims=True)
            grad_scores = (soft_weights * (grad_soft - row_inner)).astype(jnp.bfloat16)
            grad_query = jnp.einsum(
                "hqk,khd->qhd", grad_scores, key_rows, preferred_element_type=jnp.float32
            )
            keys_sum = keys_sum + jnp.einsum(
                "hqk,qhd->khd", grad_scores, query_block, preferred_element_type=jnp.float32
            )
            return (grad_query, keys_sum, values_sum)

        def skipped(operands):
            return (jnp.zeros(operands[0].shape, jnp.float32), operands[3], operands[4])

        grad_query, grad_keys, grad_values = lax.cond(
            first_row < query_limit, compute, skipped, operands
        )
        query_parts.append(grad_query)
    return (jnp.concatenate(query_parts, 0), grad_keys, grad_values)


def tile_view(matrix):
    leading = matrix.shape[:-2]
    row_count, col_count = (matrix.shape[-2], matrix.shape[-1])
    splitted = matrix.reshape(leading + (row_count // TILE, TILE, col_count // TILE, TILE))
    return jnp.swapaxes(splitted, -3, -2)


def untile(tile_grid):
    leading = tile_grid.shape[:-4]
    row_blocks, col_blocks = (tile_grid.shape[-4], tile_grid.shape[-3])
    restored = jnp.swapaxes(tile_grid, -3, -2)
    return restored.reshape(leading + (row_blocks * TILE, col_blocks * TILE))


def precondition(gradient, left_stat, right_stat, left_root, right_root, decay_rate):
    tile_grid = tile_view(gradient)
    square = tile_grid.shape
    flat_shape = square[:-2] + (TILE * TILE,)
    left_stat = left_stat.reshape(square)
    right_stat = right_stat.reshape(square)
    left_root = left_root.reshape(square)
    right_root = right_root.reshape(square)
    scaled = tile_grid * lax.rsqrt(
        jnp.mean(tile_grid * tile_grid, axis=(-2, -1), keepdims=True) + stat_eps
    )
    left_new = (
        decay_rate * left_stat
        + (1.0 - decay_rate)
        * jnp.einsum("...ij,...kj->...ik", scaled, scaled, precision=highest)
        / TILE
    )
    right_new = (
        decay_rate * right_stat
        + (1.0 - decay_rate)
        * jnp.einsum("...ji,...jk->...ik", scaled, scaled, precision=highest)
        / TILE
    )
    shaped = jnp.einsum("...ij,...jk->...ik", left_root, scaled, precision=highest)
    shaped = jnp.einsum("...ij,...jk->...ik", shaped, right_root, precision=highest)
    direction = shaped * lax.rsqrt(
        jnp.mean(shaped * shaped, axis=(-2, -1), keepdims=True) + stat_eps
    )
    return (untile(direction), left_new.reshape(flat_shape), right_new.reshape(flat_shape))


def update_gains(gradient, gain_stat, decay_rate):
    blocks = gradient.reshape(gradient.shape[0], gradient.shape[1] // TILE, TILE)
    scaled = blocks * lax.rsqrt(jnp.mean(blocks * blocks, axis=-1, keepdims=True) + stat_eps)
    stat_new = decay_rate * gain_stat.reshape(blocks.shape) + (1.0 - decay_rate) * scaled * scaled
    direction = scaled * lax.rsqrt(stat_new + stat_eps)
    return (direction.reshape(gradient.shape), stat_new.reshape(gradient.shape))


def fetch_forward(stack_in, stack_out, gain_row):
    return (
        lax.all_gather(stack_in, "fsdp", axis=1, tiled=True),
        lax.all_gather(stack_out, "fsdp", axis=1, tiled=True),
        lax.all_gather(gain_row, "fsdp", axis=0, tiled=True),
    )


def fetch_backward(stack_in, stack_out, gain_row):
    return (
        lax.all_gather(stack_in, "fsdp", axis=1, tiled=True),
        lax.all_gather(stack_out, "fsdp", axis=1, tiled=True),
        lax.all_gather(gain_row, "fsdp", axis=0, tiled=True),
    )


def reduce_parts(grad_in, grad_out_rows, grad_gain):
    return (
        lax.psum_scatter(
            grad_in.astype(jnp.bfloat16), "fsdp", scatter_dimension=1, tiled=True
        ).astype(jnp.float32),
        lax.psum_scatter(
            grad_out_rows.astype(jnp.bfloat16), "fsdp", scatter_dimension=1, tiled=True
        ).astype(jnp.float32),
        lax.psum_scatter(
            grad_gain.astype(jnp.bfloat16), "fsdp", scatter_dimension=0, tiled=True
        ).astype(jnp.float32),
    )


def body(
    home_tokens,
    home_encoder,
    out_grad,
    lengths,
    enc_lengths,
    seq_order,
    attn_master,
    ffin_master,
    ffout_master,
    gain_master,
    decays,
    attn_left,
    attn_right,
    attn_left_root,
    attn_right_root,
    ffin_left,
    ffin_right,
    ffin_left_root,
    ffin_right_root,
    ffout_left,
    ffout_right,
    ffout_left_root,
    ffout_right_root,
    gain_stats,
):
    seq_dev = out_grad.shape[1]
    total_rows = seq_dev * SEQ_LEN
    enc_rows = seq_dev * ENC_LEN
    order_row = seq_order[0]
    dealt_tokens, dealt_encoder = (
        lax.all_to_all(home_tokens[0][order_row], "fsdp", split_axis=0, concat_axis=1, tiled=True),
        lax.all_to_all(home_encoder[0][order_row], "fsdp", split_axis=0, concat_axis=1, tiled=True),
    )
    my_sequences = lax.dynamic_slice_in_dim(order_row, lax.axis_index("fsdp") * seq_dev, seq_dev)
    dec_limits = lookup(lengths[0], my_sequences)
    enc_limits = lookup(enc_lengths[0], my_sequences)
    tokens = dealt_tokens.reshape(total_rows, D).astype(jnp.float32)
    encoder = dealt_encoder.reshape(enc_rows, D)
    positions = jnp.arange(SEQ_LEN, dtype=jnp.int32)
    valid_rows = (
        (positions[None, :] < dec_limits[:, None]).astype(jnp.float32).reshape(total_rows, 1)
    )
    attn_low = attn_master.astype(jnp.bfloat16)
    ffin_low = ffin_master.astype(jnp.bfloat16)
    ffout_low = ffout_master.astype(jnp.bfloat16)[None]
    gain_low = gain_master.astype(jnp.bfloat16)
    self_in, self_out, self_gain = fetch_forward(attn_low[0:3], attn_low[3:4], gain_low[0])
    normed_one = rms_scale(tokens, self_gain.astype(jnp.float32)).astype(jnp.bfloat16)
    self_qkv = jnp.einsum(
        "rd,kde->kre", normed_one, self_in, preferred_element_type=jnp.float32
    ).astype(jnp.bfloat16)
    self_heads = self_qkv.reshape(3, seq_dev, SEQ_LEN, HEADS, HEAD)
    sequence = 0
    blended, log_total = attend_forward(
        self_heads[0, sequence],
        self_heads[1, sequence],
        self_heads[2, sequence],
        dec_limits[sequence],
        dec_limits[sequence],
        True,
    )
    self_parts_fwd = [blended]
    self_totals = [log_total]
    self_att = jnp.stack(self_parts_fwd).reshape(total_rows, D)
    hidden_one = tokens + jnp.dot(self_att, self_out[0], preferred_element_type=jnp.float32)
    cross_in, cross_out, cross_gain = fetch_forward(attn_low[4:7], attn_low[7:8], gain_low[1])
    normed_two = rms_scale(hidden_one, cross_gain.astype(jnp.float32)).astype(jnp.bfloat16)
    cross_query = jnp.dot(normed_two, cross_in[0], preferred_element_type=jnp.float32).astype(
        jnp.bfloat16
    )
    cross_kv = jnp.einsum(
        "rd,kde->kre", encoder, cross_in[1:3], preferred_element_type=jnp.float32
    ).astype(jnp.bfloat16)
    cross_query_heads = cross_query.reshape(seq_dev, SEQ_LEN, HEADS, HEAD)
    cross_kv_heads = cross_kv.reshape(2, seq_dev, ENC_LEN, HEADS, HEAD)
    sequence = 0
    blended, log_total = attend_forward(
        cross_query_heads[sequence],
        cross_kv_heads[0, sequence],
        cross_kv_heads[1, sequence],
        enc_limits[sequence],
        dec_limits[sequence],
        False,
    )
    cross_parts_fwd = [blended]
    cross_totals = [log_total]
    cross_att = jnp.stack(cross_parts_fwd).reshape(total_rows, D)
    hidden_two = hidden_one + jnp.dot(cross_att, cross_out[0], preferred_element_type=jnp.float32)
    feed_in, feed_out, feed_gain = fetch_forward(ffin_low, ffout_low, gain_low[2])
    normed_three = rms_scale(hidden_two, feed_gain.astype(jnp.float32)).astype(jnp.bfloat16)
    gate_up = jnp.einsum("rd,kdf->krf", normed_three, feed_in, preferred_element_type=jnp.float32)
    activated = gated_unit(gate_up[0], gate_up[1]).astype(jnp.bfloat16)
    result = hidden_two + jnp.einsum(
        "rf,df->rd", activated, feed_out[0], preferred_element_type=jnp.float32
    )
    out_tokens = (result * valid_rows).astype(jnp.bfloat16).reshape(1, seq_dev, SEQ_LEN, D)
    grad_result = out_grad[0].reshape(total_rows, D).astype(jnp.float32) * valid_rows
    back_in, back_out, back_gain = fetch_backward(ffin_low, ffout_low, gain_low[2])
    grad_branch = grad_result.astype(jnp.bfloat16)
    grad_feed_out = jnp.einsum(
        "rd,rf->df", grad_branch, activated, preferred_element_type=jnp.float32
    )
    grad_activated = jnp.einsum(
        "rd,df->rf", grad_branch, back_out[0], preferred_element_type=jnp.float32
    )
    unused, gate_pull = jax.vjp(gated_unit, gate_up[0], gate_up[1])
    grad_gate, grad_up = gate_pull(grad_activated)
    grad_gate_up = jnp.stack([grad_gate, grad_up]).astype(jnp.bfloat16)
    grad_feed_in = jnp.einsum(
        "rd,krf->kdf", normed_three, grad_gate_up, preferred_element_type=jnp.float32
    )
    grad_normed = jnp.einsum(
        "krf,kdf->rd", grad_gate_up, back_in, preferred_element_type=jnp.float32
    )
    unused, norm_pull = jax.vjp(rms_scale, hidden_two, back_gain.astype(jnp.float32))
    grad_hidden, grad_gain_three = norm_pull(grad_normed)
    grad_hidden_two = grad_result + grad_hidden
    feed_local = (grad_feed_in, grad_feed_out[None], grad_gain_three)
    feed_parts = reduce_parts(feed_local[0], feed_local[1], feed_local[2])
    back_cross_in, back_cross_out, back_cross_gain = fetch_backward(
        attn_low[4:7], attn_low[7:8], gain_low[1]
    )
    grad_cross_z = grad_hidden_two.astype(jnp.bfloat16)
    grad_cross_out = jnp.einsum(
        "ra,rd->ad", cross_att, grad_cross_z, preferred_element_type=jnp.float32
    )
    grad_cross_att = (
        jnp.einsum("rd,ad->ra", grad_cross_z, back_cross_out[0], preferred_element_type=jnp.float32)
        .astype(jnp.bfloat16)
        .reshape(seq_dev, SEQ_LEN, HEADS, HEAD)
    )
    query_grads = []
    key_grads = []
    value_grads = []
    sequence = 0
    grad_query, grad_keys, grad_values = attend_backward(
        cross_query_heads[sequence],
        cross_kv_heads[0, sequence],
        cross_kv_heads[1, sequence],
        cross_totals[sequence],
        grad_cross_att[sequence],
        enc_limits[sequence],
        dec_limits[sequence],
        False,
    )
    query_grads.append(grad_query)
    key_grads.append(grad_keys)
    value_grads.append(grad_values)
    grad_cross_query = jnp.stack(query_grads).reshape(total_rows, D).astype(jnp.bfloat16)
    grad_cross_kv = (
        jnp.stack([jnp.stack(key_grads), jnp.stack(value_grads)])
        .reshape(2, enc_rows, D)
        .astype(jnp.bfloat16)
    )
    grad_cross_in = jnp.concatenate(
        [
            jnp.einsum(
                "rd,re->de", normed_two, grad_cross_query, preferred_element_type=jnp.float32
            )[None],
            jnp.einsum("rd,kre->kde", encoder, grad_cross_kv, preferred_element_type=jnp.float32),
        ],
        0,
    )
    grad_normed_two = jnp.einsum(
        "re,de->rd", grad_cross_query, back_cross_in[0], preferred_element_type=jnp.float32
    )
    grad_encoder = jnp.einsum(
        "kre,kde->rd", grad_cross_kv, back_cross_in[1:3], preferred_element_type=jnp.float32
    )
    unused, norm_pull = jax.vjp(rms_scale, hidden_one, back_cross_gain.astype(jnp.float32))
    grad_hidden, grad_gain_two = norm_pull(grad_normed_two)
    grad_hidden_one = grad_hidden_two + grad_hidden
    cross_local = (grad_cross_in, grad_cross_out[None], grad_gain_two)
    cross_parts = reduce_parts(cross_local[0], cross_local[1], cross_local[2])
    back_self_in, back_self_out, back_self_gain = fetch_backward(
        attn_low[0:3], attn_low[3:4], gain_low[0]
    )
    grad_self_z = grad_hidden_one.astype(jnp.bfloat16)
    grad_self_out = jnp.einsum(
        "ra,rd->ad", self_att, grad_self_z, preferred_element_type=jnp.float32
    )
    grad_self_att = (
        jnp.einsum("rd,ad->ra", grad_self_z, back_self_out[0], preferred_element_type=jnp.float32)
        .astype(jnp.bfloat16)
        .reshape(seq_dev, SEQ_LEN, HEADS, HEAD)
    )
    query_grads = []
    key_grads = []
    value_grads = []
    sequence = 0
    grad_query, grad_keys, grad_values = attend_backward(
        self_heads[0, sequence],
        self_heads[1, sequence],
        self_heads[2, sequence],
        self_totals[sequence],
        grad_self_att[sequence],
        dec_limits[sequence],
        dec_limits[sequence],
        True,
    )
    query_grads.append(grad_query)
    key_grads.append(grad_keys)
    value_grads.append(grad_values)
    grad_self_qkv = (
        jnp.stack([jnp.stack(query_grads), jnp.stack(key_grads), jnp.stack(value_grads)])
        .reshape(3, total_rows, D)
        .astype(jnp.bfloat16)
    )
    grad_self_in = jnp.einsum(
        "rd,kre->kde", normed_one, grad_self_qkv, preferred_element_type=jnp.float32
    )
    grad_normed_one = jnp.einsum(
        "kre,kde->rd", grad_self_qkv, back_self_in, preferred_element_type=jnp.float32
    )
    unused, norm_pull = jax.vjp(rms_scale, tokens, back_self_gain.astype(jnp.float32))
    grad_hidden, grad_gain_one = norm_pull(grad_normed_one)
    grad_tokens = grad_hidden_one + grad_hidden
    self_local = (grad_self_in, grad_self_out[None], grad_gain_one)
    self_parts = reduce_parts(self_local[0], self_local[1], self_local[2])
    back_tokens, back_encoder = (
        lax.all_to_all(
            grad_tokens.astype(jnp.bfloat16).reshape(seq_dev, SEQ_LEN, D),
            "fsdp",
            split_axis=1,
            concat_axis=0,
            tiled=True,
        ),
        lax.all_to_all(
            grad_encoder.astype(jnp.bfloat16).reshape(seq_dev, ENC_LEN, D),
            "fsdp",
            split_axis=1,
            concat_axis=0,
            tiled=True,
        ),
    )
    slot_ids = jnp.arange(order_row.shape[0], dtype=jnp.int32)
    inverse = jnp.sum(
        jnp.where(order_row[None, :] == slot_ids[:, None], slot_ids[None, :], 0), axis=1
    )
    token_grad = back_tokens[inverse][None]
    encoder_grad = back_encoder[inverse][None]
    attn_grad = jnp.concatenate([self_parts[0], self_parts[1], cross_parts[0], cross_parts[1]], 0)
    ffin_grad = feed_parts[0]
    ffout_grad = feed_parts[1][0]
    gain_grad = jnp.stack([self_parts[2], cross_parts[2], feed_parts[2]])
    attn_grad, ffin_grad, ffout_grad, gain_grad = (
        lax.psum(attn_grad.astype(jnp.bfloat16), "rep").astype(jnp.float32),
        lax.psum(ffin_grad.astype(jnp.bfloat16), "rep").astype(jnp.float32),
        lax.psum(ffout_grad.astype(jnp.bfloat16), "rep").astype(jnp.float32),
        lax.psum(gain_grad.astype(jnp.bfloat16), "rep").astype(jnp.float32),
    )
    attn_update, attn_left_new, attn_right_new = precondition(
        attn_grad, attn_left, attn_right, attn_left_root, attn_right_root, decays[0]
    )
    ffin_update, ffin_left_new, ffin_right_new = precondition(
        ffin_grad, ffin_left, ffin_right, ffin_left_root, ffin_right_root, decays[1]
    )
    ffout_update, ffout_left_new, ffout_right_new = precondition(
        ffout_grad, ffout_left, ffout_right, ffout_left_root, ffout_right_root, decays[2]
    )
    gain_update, gain_stats_new = update_gains(gain_grad, gain_stats, decays[3])
    return (
        out_tokens,
        token_grad,
        encoder_grad,
        attn_grad,
        ffin_grad,
        ffout_grad,
        gain_grad,
        attn_update,
        ffin_update,
        ffout_update,
        gain_update,
        attn_left_new,
        attn_right_new,
        ffin_left_new,
        ffin_right_new,
        ffout_left_new,
        ffout_right_new,
        gain_stats_new,
    )


def solution(mesh):
    in_specs = (
        P("rep", None, "fsdp", None),
        P("rep", None, "fsdp", None),
        P("rep", "fsdp", None, None),
        P("rep", None),
        P("rep", None),
        P("rep", None),
        P(None, "fsdp", None),
        P(None, "fsdp", None),
        P("fsdp", None),
        P(None, "fsdp"),
        P(),
        P(None, "fsdp", None, None),
        P(None, "fsdp", None, None),
        P(None, "fsdp", None, None),
        P(None, "fsdp", None, None),
        P(None, "fsdp", None, None),
        P(None, "fsdp", None, None),
        P(None, "fsdp", None, None),
        P(None, "fsdp", None, None),
        P("fsdp", None, None),
        P("fsdp", None, None),
        P("fsdp", None, None),
        P("fsdp", None, None),
        P(None, "fsdp"),
    )
    out_specs = (
        P("rep", "fsdp", None, None),
        P("rep", None, "fsdp", None),
        P("rep", None, "fsdp", None),
        P(None, "fsdp", None),
        P(None, "fsdp", None),
        P("fsdp", None),
        P(None, "fsdp"),
        P(None, "fsdp", None),
        P(None, "fsdp", None),
        P("fsdp", None),
        P(None, "fsdp"),
        P(None, "fsdp", None, None),
        P(None, "fsdp", None, None),
        P(None, "fsdp", None, None),
        P(None, "fsdp", None, None),
        P("fsdp", None, None),
        P("fsdp", None, None),
        P(None, "fsdp"),
    )
    return jax.shard_map(body, mesh=mesh, in_specs=in_specs, out_specs=out_specs, check_vma=False)
```

profile of v0, /device:TPU:0, one launch (start us, length us, event | category | flops | bytes accessed | tf_op | source)
XLA Modules:
  0.0 1747.4 jit_solution(15487933213921147702)
XLA Ops:
  34.5 70.6 %all-gather = bf16[1,1024]{1,0:T(2,128)(2,1)S(1)} all-gather(bf16[1,128]{1,0:T(2,128)(2,1)S(1)} %get-tuple-element.592), channel_id=2, replica_groups=mesh['rep'=4,'fsdp'=8] {'fsdp'}, dimensions={1}, use_global_device_ids=true | all-gather | bytes 2304 | tf_op jit(solution)/shard_map/all_gather | solution.py:194
  105.1 29.5 %all-gather.1 = bf16[1,1024]{1,0:T(2,128)(2,1)S(1)} all-gather(bf16[1,128]{1,0:T(2,128)(2,1)S(1)} %get-tuple-element.591), channel_id=3, replica_groups=mesh['rep'=4,'fsdp'=8] {'fsdp'}, dimensions={1}, use_global_device_ids=true | all-gather | bytes 2304 | tf_op jit(solution)/shard_map/all_gather | solution.py:194
  184.3 29.2 %all-to-all-done.1 = bf16[8,64,1024]{2,1,0:T(8,128)(2,1)} async-done(((bf16[8,64,1024]{2,1,0:T(8,128)(2,1)}), bf16[8,64,1024]{2,1,0:T(8,128)(2,1)}, u32[]{:S(2)}, u32[]{:S(2)}) %all-to-all-start.1) | async-done | bytes 1048608 | tf_op jit(solution)/shard_map/all_to_all | solution.py:252
  226.4 43.8 %conditional.9 = (bf16[512,16,64]{0,2,1:T(8,128)(2,1)S(1)}, f32[16,512]{1,0:T(8,128)S(1)}) conditional(s32[]{:T(128)} %convert_element_type.271, () %tuple.74, (s32[]{:T(128)}, bf16[512,16,64]{0,2,1:T(8,128)(2,1)S(1)}, bf16[1024,16,64]{0,2,1:T(8,128)(2,1)S(1)}, bf16[1024,16,64]{0,2,1:T(8,128)(2,1)}) %tuple.224), branch_computations={%region_6.7_spmd, %region_7.0_spmd} | conditional | flops 2224547328 | bytes 117708848 | solution.py:83
  271.2 46.2 %conditional.8 = (bf16[512,16,64]{0,2,1:T(8,128)(2,1)S(1)}, f32[16,512]{1,0:T(8,128)S(1)}) conditional(s32[]{:T(128)} %convert_element_type.263, () %tuple.72, (s32[]{:T(128)}, bf16[512,16,64]{0,2,1:T(8,128)(2,1)}, bf16[1024,16,64]{0,2,1:T(8,128)(2,1)S(1)}, bf16[1024,16,64]{0,2,1:T(8,128)(2,1)}) %tuple.226), branch_computations={%region_2.3_spmd, %region_3.6_spmd} | conditional | flops 2224546816 | bytes 117704752 | solution.py:83
  333.1 26.6 %conditional.11 = (bf16[512,16,64]{0,2,1:T(8,128)(2,1)S(1)}, f32[16,512]{1,0:T(8,128)S(1)}) conditional(s32[]{:T(128)} %convert_element_type.271, () %tuple.78, (s32[]{:T(128)}, bf16[512,16,64]{0,2,1:T(8,128)(2,1)}, bf16[512,16,64]{0,2,1:T(8,128)(2,1)S(1)}, bf16[512,16,64]{0,2,1:T(8,128)(2,1)S(1)}) %tuple.230), branch_computations={%region_16.17_spmd, %region_17.20_spmd} | conditional | flops 1112007168 | bytes 54790164 | solution.py:83
  360.6 26.5 %conditional.10 = (bf16[512,16,64]{0,2,1:T(8,128)(2,1)}, f32[16,512]{1,0:T(8,128)S(1)}) conditional(s32[]{:T(128)} %convert_element_type.263, () %tuple.76, (s32[]{:T(128)}, bf16[512,16,64]{0,2,1:T(8,128)(2,1)S(1)}, bf16[512,16,64]{0,2,1:T(8,128)(2,1)S(1)}, bf16[512,16,64]{0,2,1:T(8,128)(2,1)S(1)}) %tuple.231), branch_computations={%region_12.13_spmd, %region_13.16_spmd} | conditional | flops 1112007168 | bytes 54790164 | solution.py:83
  398.2 21.0 %convolution_bitcast_fusion.2 = f32[2,1024,2816]{2,1,0:T(8,128)} fusion(bf16[2,1024,2816]{2,1,0:T(8,128)(2,1)} %all-gather.19.cloned.1.call-done, f32[1024,1024]{0,1:T(8,128)} %get-tuple-element.600, f32[1024]{0:T(1024)S(1)} %bitcast.501, f32[1024]{0:T(1024)S(1)} %fusion.179), kind=kOutput, calls=%fused_computation.133 | convolution fusion | flops 11814305792 | bytes 38805504 | tf_op jit(solution)/shard_map/rd,kdf->krf/dot_general | solution.py:311
  419.1 28.9 %all-gather.21.cloned.1.call-done = bf16[1024,2816]{1,0:T(8,128)(2,1)} async-done(((bf16[128,2816]{1,0:T(8,128)(2,1)}), bf16[1024,2816]{1,0:T(8,128)(2,1)}) %all-gather.21.cloned.1.call-update) | async-done | bytes 5767184 | tf_op jit(solution)/shard_map/all_gather | solution.py:193
  448.0 27.1 %fusion.91 = (bf16[1,1024,2816]{2,1,0:T(8,128)(2,1)}, bf16[1,1024,2816]{2,1,0:T(8,128)(2,1)}) fusion(f32[2,1024,2816]{2,1,0:T(8,128)} %convolution_bitcast_fusion.2, bf16[1024,2816]{1,0:T(8,128)(2,1)} %all-gather.21.cloned.1.call-done, bf16[1,1,1024,1024]{2,3,1,0:T(8,128)(2,1)} %copy.556, f32[1024]{0:T(1024)S(1)} %copy-done.64), kind=kOutput, calls=%fused_computation.168 | convolution fusion | flops 5989466112 | bytes 42471424 | tf_op jit(solution)/shard_map/rd,df->rf/dot_general | solution.py:323
  475.1 23.4 %fusion.104 = (bf16[1024]{0:T(1024)(128)(2,1)}, f32[1024]{0:T(1024)S(1)}, f32[1024,1024,1]{0,1,2:T(8,128)}) fusion(f32[1024,1024]{0,1:T(8,128)} %get-tuple-element.600, f32[1024]{0:T(1024)S(1)} %fusion.179, f32[1024]{0:T(1024)S(1)} %bitcast.502, bf16[2,1024,2816]{2,1,0:T(8,128)(2,1)} %all-gather.19.cloned.1.call-done, ...), kind=kOutput, calls=%fused_computation.187 | convolution fusion | flops 11823216640 | bytes 31471616 | tf_op jit(solution)/shard_map/krf,kdf->rd/dot_general | solution.py:332
  518.5 64.1 %conditional.12 = (f32[512,16,64]{0,2,1:T(8,128)}, f32[512,16,64]{0,2,1:T(8,128)}, bf16[512,16,64]{0,2,1:T(8,128)(2,1)}, bf16[512,1024]{0,1:T(8,128)(2,1)S(1)}) conditional(s32[]{:T(128)} %convert_element_type.263, () %tuple.80, (s32[]{:T(128)}, bf16[512,16,64]{0,2,1:T(8,128)(2,1)S(1)}, bf16[512,16,64]{0,2,1:T(8,128)(2,1)S(1)}, ...), branch_computations={%region_22.23_spmd, %region_23.25_spmd} | conditional | flops 2735202816 | bytes 184715360 | solution.py:130
  583.6 65.2 %conditional.13 = (f32[512,16,64]{0,2,1:T(8,128)}, f32[512,16,64]{0,2,1:T(8,128)}, bf16[512,16,64]{0,2,1:T(8,128)(2,1)}, bf16[512,1024]{0,1:T(8,128)(2,1)S(1)}) conditional(s32[]{:T(128)} %convert_element_type.271, (f32[512,16,64]{0,2,1:T(8,128)}, f32[512,16,64]{0,2,1:T(8,128)}) %tuple.82, (s32[]{:T(128)}, bf16[512,16,64]{0,2,1:T(8,128)(2,1)}, ...), branch_computations={%region_25.26_spmd, %region_26.28_spmd} | conditional | flops 2736251392 | bytes 184715328 | solution.py:130
  720.7 111.5 %conditional.14 = (f32[1024,16,64]{0,2,1:T(8,128)}, f32[1024,16,64]{0,2,1:T(8,128)}, bf16[512,16,64]{0,2,1:T(8,128)(2,1)}) conditional(s32[]{:T(128)} %convert_element_type.263, () %tuple.84, (s32[]{:T(128)}, bf16[512,16,64]{0,2,1:T(8,128)(2,1)S(1)}, bf16[1024,16,64]{0,2,1:T(8,128)(2,1)S(1)}, f32[16,512]{1,0:T(8,128)S(1)}, ...), branch_computations={%region_29.30_spmd, %region_30.32_spmd} | conditional | flops 5470938112 | bytes 303204544 | solution.py:130
  742.1 24.9 %multiply_reduce_fusion.2 = (f32[16,512]{1,0:T(8,128)S(1)}, f32[16,512,1024]{2,1,0:T(8,128)}) fusion(f32[16,512,1024]{2,1,0:T(8,128)} %fusion.205, f32[16,512]{1,0:T(8,128)S(1)} %get-tuple-element.139, pred[512,1024]{1,0:T(8,128)(4,1)} %fusion.50, bf16[512,16,64]{0,2,1:T(8,128)(2,1)S(1)} %bitcast.460, bf16[1024,16,64]{0,2,1:T(8,128)(2,1)S(1)} %copy-done.11), kind=kOutput, calls=%fused_computation.76 | convolution fusion | flops 1107288064 | bytes 70844416 | tf_op jit(solution)/shard_map/cond/branch_1_fun/qhd,khd->hqk/dot_general | solution.py:108
  767.0 28.4 %multiply_convert_fusion.2 = bf16[16,512,1024]{2,1,0:T(8,128)(2,1)} fusion(f32[16,512,1024]{2,1,0:T(8,128)} %get-tuple-element.573, f32[16,512,1024]{2,1,0:T(8,128)} %fusion.205, f32[16,512]{1,0:T(8,128)S(1)} %get-tuple-element.572, f32[16,512]{1,0:T(8,128)S(1)} %get-tuple-element.139, pred[512,1024]{1,0:T(8,128)(4,1)} %fusion.50), kind=kLoop, calls=%fused_computation.75 | loop fusion | flops 41943040 | bytes 84475904 | tf_op jit(solution)/shard_map/cond/branch_1_fun/convert_element_type | solution.py:118
  832.2 114.3 %conditional.15 = (f32[1024,16,64]{0,2,1:T(8,128)}, f32[1024,16,64]{0,2,1:T(8,128)}, bf16[512,16,64]{0,2,1:T(8,128)(2,1)}) conditional(s32[]{:T(128)} %convert_element_type.271, (f32[1024,16,64]{0,2,1:T(8,128)}, f32[1024,16,64]{0,2,1:T(8,128)}) %tuple.86, (s32[]{:T(128)}, bf16[512,16,64]{0,2,1:T(8,128)(2,1)S(1)}, ...), branch_computations={%region_32.33_spmd, %region_33.35_spmd} | conditional | flops 5473035776 | bytes 301111392 | solution.py:130
  853.3 24.7 %multiply_reduce_fusion.3 = (f32[16,512]{1,0:T(8,128)S(1)}, f32[16,512,1024]{2,1,0:T(8,128)}) fusion(f32[16,512,1024]{2,1,0:T(8,128)} %fusion.206, f32[16,512]{1,0:T(8,128)S(1)} %get-tuple-element.147, pred[512,1024]{1,0:T(8,128)(4,1)} %fusion.61, bf16[512,16,64]{0,2,1:T(8,128)(2,1)S(1)} %bitcast.458, bf16[1024,16,64]{0,2,1:T(8,128)(2,1)S(1)} %copy-done.12), kind=kOutput, calls=%fused_computation.92 | convolution fusion | flops 1107288064 | bytes 70844416 | tf_op jit(solution)/shard_map/cond/branch_1_fun/qhd,khd->hqk/dot_general | solution.py:108
  878.0 28.0 %multiply_convert_fusion.3 = bf16[16,512,1024]{2,1,0:T(8,128)(2,1)} fusion(f32[16,512,1024]{2,1,0:T(8,128)} %get-tuple-element.575, f32[16,512,1024]{2,1,0:T(8,128)} %fusion.206, f32[16,512]{1,0:T(8,128)S(1)} %get-tuple-element.574, f32[16,512]{1,0:T(8,128)S(1)} %get-tuple-element.147, pred[512,1024]{1,0:T(8,128)(4,1)} %fusion.61), kind=kLoop, calls=%fused_computation.91 | loop fusion | flops 41943040 | bytes 84475904 | tf_op jit(solution)/shard_map/cond/branch_1_fun/convert_element_type | solution.py:118
  998.9 19.4 %convert_bitcast_fusion = bf16[2,1024,2816]{1,2,0:T(8,128)(2,1)} fusion(bf16[1,1024,2816]{2,1,0:T(8,128)(2,1)} %get-tuple-element.577, bf16[1,1024,2816]{2,1,0:T(8,128)(2,1)} %get-tuple-element.576, f32[1024,1024]{0,1:T(8,128)} %get-tuple-element.600, f32[1024]{0:T(1024)S(1)} %bitcast.504, f32[1024]{0:T(1024)S(1)} %copy-done.71), kind=kOutput, calls=%fused_computation.131 | convolution fusion | flops 11825840128 | bytes 27271168 | tf_op jit(solution)/shard_map/rd,krf->kdf/dot_general | solution.py:329
  1018.3 29.0 %copy.679 = bf16[2,1024,2816]{2,0,1:T(2,128)(2,1)} copy(bf16[2,1024,2816]{1,2,0:T(8,128)(2,1)} %convert_bitcast_fusion) | data formatting | bytes 23068672
  1166.0 37.8 %reduce-scatter.27.cloned.1.call-done = bf16[128,5632]{1,0:T(8,128)(2,1)} async-done(((bf16[1024,5632]{1,0:T(8,128)(2,1)}), bf16[128,5632]{1,0:T(8,128)(2,1)}) %reduce-scatter.27.cloned.1.call-update) | async-done | bytes 1441808
  1210.3 63.6 %reduce-scatter.17.cloned.1.call-done = bf16[1,128,2816]{2,1,0:T(8,128)(2,1)} async-done(((bf16[1,1024,2816]{2,1,0:T(8,128)(2,1)}), bf16[1,128,2816]{2,1,0:T(8,128)(2,1)}) %reduce-scatter.17.cloned.1.call-update) | async-done | bytes 720912 | tf_op jit(solution)/shard_map/reduce_scatter | solution.py:211
  1609.8 22.1 %multiply_add_fusion.4 = f32[8,2,16,64,64]{4,3,2,1,0:T(8,128)} fusion(f32[8,2,16,64,64]{4,3,2,1,0:T(8,128)} %mul.627, f32[]{:T(128)S(6)} %sub.116, f32[8,2,16,64,64]{4,3,2,1,0:T(8,128)} %copy.606), kind=kOutput, calls=%fused_computation.135 | convolution fusion | flops 808452096 | bytes 12582916 | tf_op jit(solution)/shard_map/...ij,...kj->...ik/dot_general | solution.py:165
  (473 shorter events, 1216.9 us)
Async XLA Ops:
  7.2 163.8 %all-gather.11.cloned.1.call-start = ((), (), s32[]{:S(2)}) async-start(), calls=%async_computation.10 | async-start | bytes 7077888 | tf_op jit(solution)/shard_map/all_gather | solution.py:192
  14.6 200.8 %all-gather.15.cloned.1.call-start = ((), (), s32[]{:S(2)}) async-start(), calls=%async_computation.12 | async-start | bytes 7077888 | tf_op jit(solution)/shard_map/all_gather | solution.py:192
  15.4 304.2 %all-gather.13.cloned.1.call-start = ((), (), s32[]{:S(2)}) async-start(), calls=%async_computation.11 | async-start | bytes 2359296 | tf_op jit(solution)/shard_map/all_gather | solution.py:193
  17.3 373.0 %all-gather.17.cloned.1.call-start = ((), (), s32[]{:S(2)}) async-start(), calls=%async_computation.13 | async-start | bytes 2359296 | tf_op jit(solution)/shard_map/all_gather | solution.py:193
  17.9 380.2 %all-gather.19.cloned.1.call-start = ((), (), s32[]{:S(2)}) async-start(), calls=%async_computation.14 | async-start | bytes 12976128 | tf_op jit(solution)/shard_map/all_gather | solution.py:192
  23.1 131.7 %all-to-all-start = ((bf16[8,128,1024]{2,1,0:T(8,128)(2,1)}), bf16[8,128,1024]{2,1,0:T(8,128)(2,1)S(1)}, u32[]{:S(2)}, u32[]{:S(2)}) async-start(bf16[8,128,1024]{2,1,0:T(8,128)(2,1)} %gather_fusion), calls=%async_computation | async-start | bytes 4194304 | tf_op jit(solution)/shard_map/all_to_all | solution.py:251
  29.6 123.9 %copy-start.86 = (s32[1,8]{1,0:T(1,128)S(1)}, s32[1,8]{1,0:T(1,128)}, u32[]{:S(2)}) copy-start(s32[1,8]{1,0:T(1,128)} %param.44) | copy-start | bytes 100
  29.6 418.4 %all-gather.21.cloned.1.call-start = ((), (), s32[]{:S(2)}) async-start(), calls=%async_computation.16 | async-start | bytes 6488064 | tf_op jit(solution)/shard_map/all_gather | solution.py:193
  154.7 58.8 %all-to-all-start.1 = ((bf16[8,64,1024]{2,1,0:T(8,128)(2,1)}), bf16[8,64,1024]{2,1,0:T(8,128)(2,1)}, u32[]{:S(2)}, u32[]{:S(2)}) async-start(bf16[8,64,1024]{2,1,0:T(8,128)(2,1)} %gather_fusion.1), calls=%async_computation.1 | async-start | bytes 2097152 | tf_op jit(solution)/shard_map/all_to_all | solution.py:252
  166.8 985.1 %reduce-scatter.25.cloned.1.call-start = ((), (), s32[]{:S(2)}) async-start(), calls=%async_computation.20 | async-start | bytes 2359296
  184.3 86.0 %copy-start.4 = (bf16[1,1024,1024]{1,2,0:T(8,128)(2,1)}, bf16[1,1024,1024]{1,2,0:T(8,128)(2,1)S(1)}, u32[]{:S(2)}) copy-start(bf16[1,1024,1024]{1,2,0:T(8,128)(2,1)S(1)} %get-tuple-element.581) | copy-start | bytes 6291460
  398.1 100.4 %copy-start.70 = (f32[1024]{0:T(1024)}, f32[1024]{0:T(1024)S(1)}, u32[]{:S(2)}) copy-start(f32[1024]{0:T(1024)S(1)} %fusion.179) | copy-start | bytes 12292
  511.9 641.8 %reduce-scatter.21.cloned.1.call-start = ((), (), s32[]{:S(2)}) async-start(), calls=%async_computation.18 | async-start | bytes 2359296
  582.6 66.2 %copy-start.69 = (f32[1,1024]{1,0:T(1,128)S(1)}, f32[1,1024]{1,0:T(1,128)}, u32[]{:S(2)}) copy-start(f32[1,1024]{1,0:T(1,128)} %convert_element_type.318) | copy-start | bytes 12292
  582.6 66.2 %copy-start.73 = (f32[1024]{0:T(1024)S(1)}, f32[1024]{0:T(1024)}, u32[]{:S(2)}) copy-start(f32[1024]{0:T(1024)} %copy-done.72) | copy-start | bytes 12292
  666.8 488.6 %reduce-scatter.23.cloned.1.call-start = ((), (), s32[]{:S(2)}) async-start(), calls=%async_computation.19 | async-start | bytes 7077888
  713.9 445.1 %reduce-scatter.19.cloned.1.call-start = ((), (), s32[]{:S(2)}) async-start(), calls=%async_computation.17 | async-start | bytes 7077888
  720.7 111.5 %copy-start.14 = (bf16[1,512,1024]{1,2,0:T(8,128)(2,1)S(1)}, bf16[1,512,1024]{1,2,0:T(8,128)(2,1)}, u32[]{:S(2)}) copy-start(bf16[1,512,1024]{1,2,0:T(8,128)(2,1)} %copy-done.13) | copy-start | bytes 3145732
  720.7 111.5 %copy-start.53 = (f32[16,512]{1,0:T(8,128)S(1)}, f32[16,512]{1,0:T(8,128)}, u32[]{:S(2)}) copy-start(f32[16,512]{1,0:T(8,128)} %copy-done.52) | copy-start | bytes 98308
  998.2 205.5 %reduce-scatter.27.cloned.1.call-start = ((), (), s32[]{:S(2)}) async-start(), calls=%async_computation.21 | async-start | bytes 12976128
  1058.7 215.1 %reduce-scatter.17.cloned.1.call-start = ((), (), s32[]{:S(2)}) async-start(), calls=%async_computation.15 | async-start | bytes 6488064 | tf_op jit(solution)/shard_map/reduce_scatter | solution.py:211
  1109.9 164.0 %all-to-all-start.3 = ((bf16[8,2,32768]{2,1,0:T(2,128)(2,1)}), bf16[8,2,32768]{2,1,0:T(2,128)(2,1)S(1)}, u32[]{:S(2)}, u32[]{:S(2)}) async-start(bf16[8,2,32768]{2,1,0:T(2,128)(2,1)} %reshape.715), calls=%async_computation.3 | async-start | bytes 2097152 | tf_op jit(solution)/shard_map/all_to_all | solution.py:448
  1113.4 305.8 %all-reduce.7.cloned.1.call-start = ((), (), s32[]{:S(2)}) async-start(), calls=%async_computation.22 | async-start | bytes 8519680 | tf_op jit(solution)/shard_map/psum | solution.py:467
  1273.9 136.0 %all-to-all-start.2 = ((bf16[8,2,65536]{2,1,0:T(2,128)(2,1)}), bf16[8,2,65536]{2,1,0:T(2,128)(2,1)S(1)}, u32[]{:S(2)}, u32[]{:S(2)}) async-start(bf16[8,2,65536]{2,1,0:T(2,128)(2,1)} %reshape.713), calls=%async_computation.2 | async-start | bytes 4194304 | tf_op jit(solution)/shard_map/all_to_all | solution.py:441
  (81 other events, 765.2 us)
Sparse Core Ops, SparseCore 0:
  14.8 112.2 all-gather.10
  129.2 86.1 all-gather.14
  217.6 28.7 all-gather.12
  248.4 29.6 all-gather.16
  280.2 107.0 all-gather.18
  389.3 58.6 all-gather.20
  512.0 34.7 reduce-scatter.24
  666.9 34.6 reduce-scatter.20
  714.0 68.4 reduce-scatter.22
  998.4 68.4 reduce-scatter.18
  1069.2 134.5 reduce-scatter.26
  1205.9 67.8 reduce-scatter.16
  1278.7 103.3 all-reduce.6
where the time goes:
time: 1760 us; the launch traced here: 1750 us
  matrix products  682 us (39%)
  local copies, waits for them, and re-layouts  449 us (26%)
  other arithmetic  266 us (15%)
  waiting for transfers between devices  163 us (9%)
  blocking collectives  137 us (8%)
  starting transfers between devices  26.8 us (2%)
  between operations  19.8 us (1%)
    unnamed x189, local copies, waits for them, and re-layouts  190 us
    all_gather x3, blocking collectives, fetch_forward(): lax.all_gather(gain_row, 'fsdp', axis=0, tiled=True)  110 us
    dot_general x8, matrix products, block_scores(): jnp.einsum('qhd,khd->hqk', query_block, key_rows, preferred_element_type=...  89.5 us
    convert_element_type x4, other arithmetic, compute(): grad_scores = (soft_weights * (grad_soft - row_inner)).astype(jnp.bfloat16)  80.9 us
    dot_general x4, matrix products, compute(): jnp.einsum('qhd,khd->hqk', grad_block, value_rows, preferred_element_type...  74.1 us
    reduce_scatter x1, waiting for transfers between devices, reduce_parts(): lax.psum_scatter(grad_out_rows.astype(jnp.bfloat16), 'fsdp', scatter_dime...  63.6 us
    dot_general x4, matrix products, compute(): jnp.einsum('hqk,qhd->khd', soft_weights.astype(jnp.bfloat16), grad_block,...  54.9 us
    reduce_sum x4, other arithmetic, compute(): row_total = jnp.sum(exp_scores, axis=-1, keepdims=True)  48.1 us
  transfers between devices with their start and end apart: 17, of which 5 were waited for; matrix products, arithmetic and copies ran while one was open for 57% of the time, Pallas kernels for 0%

commit v1 on v0

v1 whole, which is shorter than its diff:
```python
import functools

import jax
import jax.numpy as jnp
from jax import lax
from jax.experimental import pallas as pl
from jax.experimental.pallas import tpu as pltpu
from jax.sharding import PartitionSpec as P

D = 1024
HEADS = 16
HEAD = 64
TILE = 64
SEQ_LEN = 1024
ENC_LEN = 512


norm_eps = 1e-06
stat_eps = 1e-06
masked_score = -1e30


def rms_scale(inputs, gain_row):
    return (
        inputs * lax.rsqrt(jnp.mean(inputs * inputs, axis=-1, keepdims=True) + norm_eps) * gain_row
    )


def gelu_tanh(inputs):
    return (
        0.5
        * inputs
        * (1.0 + jnp.tanh(0.7978845608 * (inputs + 0.044715 * inputs * inputs * inputs)))
    )


def gated_unit(gate_part, up_part):
    return gelu_tanh(gate_part) * up_part


def lookup(table_row, chosen):
    slot_ids = jnp.arange(table_row.shape[0], dtype=jnp.int32)
    return jnp.sum(jnp.where(chosen[:, None] == slot_ids[None, :], table_row[None, :], 0), axis=1)


def update_gains(gradient, gain_stat, decay_rate):
    blocks = gradient.reshape(gradient.shape[0], gradient.shape[1] // TILE, TILE)
    scaled = blocks * lax.rsqrt(jnp.mean(blocks * blocks, axis=-1, keepdims=True) + stat_eps)
    stat_new = decay_rate * gain_stat.reshape(blocks.shape) + (1.0 - decay_rate) * scaled * scaled
    direction = scaled * lax.rsqrt(stat_new + stat_eps)
    return (direction.reshape(gradient.shape), stat_new.reshape(gradient.shape))


PAIR = 2 * HEAD
ROWS_Q = 256
KEYS_B = 256
NT = (((1,), (1,)), ((), ()))


def matmul(left_side, right_side, dims=(((1,), (0,)), ((), ()))):
    return lax.dot_general(left_side, right_side, dims, preferred_element_type=jnp.float32)


def lane_half(values, which):
    lanes = lax.broadcasted_iota(jnp.int32, values.shape, len(values.shape) - 1)
    return jnp.where((lanes < HEAD) == (which == 0), values, jnp.zeros_like(values))


def masked(scores, key_start, query_start, limit, causal):
    key_pos = key_start + lax.broadcasted_iota(jnp.int32, scores.shape, 0)
    allowed = key_pos < limit
    if causal:
        query_pos = query_start + lax.broadcasted_iota(jnp.int32, scores.shape, 1)
        allowed = allowed & (key_pos <= query_pos)
    return jnp.where(allowed, scores, masked_score)


def forward_kernel(causal, limit_ref, q_ref, k_ref, v_ref, o_ref, total_ref, vt_ref):
    limit = limit_ref[0]
    query_count, key_count = (q_ref.shape[0], k_ref.shape[0])
    vt_ref[...] = v_ref[...].T
    for first in range(0, query_count, ROWS_Q):
        span = min(first + ROWS_Q, key_count) if causal else key_count
        queries = q_ref[first : first + ROWS_Q, :]
        halves = []
        for which in range(2):
            picked = lane_half(queries, which)
            pieces = []
            for start in range(0, span, KEYS_B):
                piece = matmul(k_ref[start : start + KEYS_B, :], picked, NT)
                diagonal = causal and start + KEYS_B > first
                pieces.append(masked(piece, start, first, limit, diagonal))
            top = pieces[0].max(axis=0, keepdims=True)
            for piece in pieces[1:]:
                top = jnp.maximum(top, piece.max(axis=0, keepdims=True))
            total = jnp.zeros_like(top)
            blended = jnp.zeros((HEAD, ROWS_Q), jnp.float32)
            for number, piece in enumerate(pieces):
                weights = jnp.exp(piece - top)
                total = total + weights.sum(axis=0, keepdims=True)
                start = number * KEYS_B
                blended = blended + matmul(
                    vt_ref[which * HEAD : (which + 1) * HEAD, start : start + KEYS_B],
                    weights.astype(jnp.bfloat16),
                )
            halves.append(blended / total)
            total_ref[which : which + 1, first : first + ROWS_Q] = top + jnp.log(total)
        o_ref[first : first + ROWS_Q, :] = jnp.concatenate(halves, 0).T.astype(o_ref.dtype)


def backward_kernel(
    causal, parts, limit_ref, q_ref, k_ref, v_ref, o_ref, g_ref, total_ref, *rest
):
    outs, (dqt_ref, kt_ref, inner_ref) = (rest[:-3], rest[-3:])
    limit = limit_ref[0]
    query_count, key_count = (q_ref.shape[0], k_ref.shape[0])
    kt_ref[...] = k_ref[...].T
    for first in range(0, query_count, ROWS_Q):
        both = g_ref[first : first + ROWS_Q, :].astype(jnp.float32) * o_ref[
            first : first + ROWS_Q, :
        ].astype(jnp.float32)
        turned = both.T
        for which in range(2):
            inner_ref[which : which + 1, first : first + ROWS_Q] = turned[
                which * HEAD : (which + 1) * HEAD, :
            ].sum(axis=0, keepdims=True)
    dqt_ref[...] = jnp.zeros_like(dqt_ref)
    for start in range(0, key_count, KEYS_B):
        key_block = k_ref[start : start + KEYS_B, :]
        value_block = v_ref[start : start + KEYS_B, :]
        key_sum = jnp.zeros((KEYS_B, PAIR), jnp.float32)
        value_sum = jnp.zeros((KEYS_B, PAIR), jnp.float32)
        for first in range(start if causal else 0, query_count, ROWS_Q):
            rows = slice(first, first + ROWS_Q)
            for which in range(2):
                picked = lane_half(q_ref[rows, :], which)
                pulled = lane_half(g_ref[rows, :], which)
                scores = masked(
                    matmul(key_block, picked, NT), start, first, limit, causal and start == first
                )
                weights = jnp.exp(scores - total_ref[which : which + 1, rows])
                value_sum = value_sum + matmul(weights.astype(jnp.bfloat16), pulled)
                slopes = matmul(value_block, pulled, NT) - inner_ref[which : which + 1, rows]
                slopes = (weights * slopes).astype(jnp.bfloat16)
                key_sum = key_sum + matmul(slopes, picked)
                feats = slice(which * HEAD, (which + 1) * HEAD)
                dqt_ref[feats, rows] += matmul(kt_ref[feats, start : start + KEYS_B], slopes)
        parts(outs, start, key_sum, value_sum)
    return dqt_ref


def attention_forward(queries, keys, limit, q_at, k_at, v_at, causal):
    rows, key_rows = (queries.shape[0], keys.shape[0])
    pairs = D // PAIR
    grid_spec = pltpu.PrefetchScalarGridSpec(
        num_scalar_prefetch=1,
        grid=(pairs,),
        in_specs=[
            pl.BlockSpec((rows, PAIR), lambda p, _: (0, q_at * pairs + p)),
            pl.BlockSpec((key_rows, PAIR), lambda p, _: (0, k_at * pairs + p)),
            pl.BlockSpec((key_rows, PAIR), lambda p, _: (0, v_at * pairs + p)),
        ],
        out_specs=[
            pl.BlockSpec((rows, PAIR), lambda p, _: (0, p)),
            pl.BlockSpec((None, 8, rows), lambda p, _: (p, 0, 0)),
        ],
        scratch_shapes=[pltpu.VMEM((PAIR, key_rows), jnp.bfloat16)],
    )
    pixels = rows * key_rows * HEADS * (0.625 if causal else 1.0)
    return pl.pallas_call(
        functools.partial(forward_kernel, causal),
        grid_spec=grid_spec,
        out_shape=(
            jax.ShapeDtypeStruct((rows, D), jnp.bfloat16),
            jax.ShapeDtypeStruct((pairs, 8, rows), jnp.float32),
        ),
        cost_estimate=pl.CostEstimate(
            flops=int(pixels * 512 * 2), bytes_accessed=rows * D * 8, transcendentals=int(pixels)
        ),
    )(limit, queries, keys, keys)


def self_back(limit_ref, q_ref, k_ref, v_ref, o_ref, g_ref, total_ref, out_ref, dk_ref, dv_ref, *scratch):
    turn = pl.program_id(1)

    @pl.when(turn == 0)
    def compute():
        def keep(outs, start, key_sum, value_sum):
            dk_ref[start : start + KEYS_B, :] = key_sum.astype(jnp.bfloat16)
            dv_ref[start : start + KEYS_B, :] = value_sum.astype(jnp.bfloat16)

        dqt_ref = backward_kernel(
            True, keep, limit_ref, q_ref, k_ref, v_ref, o_ref, g_ref, total_ref, *scratch
        )
        out_ref[...] = dqt_ref[...].T.astype(jnp.bfloat16)

    @pl.when(turn == 1)
    def give_keys():
        out_ref[...] = dk_ref[...]

    @pl.when(turn == 2)
    def give_values():
        out_ref[...] = dv_ref[...]


def cross_back(limit_ref, q_ref, k_ref, v_ref, o_ref, g_ref, total_ref, dq_ref, kv_ref, dv_ref, *scratch):
    turn = pl.program_id(1)

    @pl.when(turn == 0)
    def compute():
        def keep(outs, start, key_sum, value_sum):
            kv_ref[start : start + KEYS_B, :] = key_sum.astype(jnp.bfloat16)
            dv_ref[start : start + KEYS_B, :] = value_sum.astype(jnp.bfloat16)

        dqt_ref = backward_kernel(
            False, keep, limit_ref, q_ref, k_ref, v_ref, o_ref, g_ref, total_ref, *scratch
        )
        dq_ref[...] = dqt_ref[...].T.astype(jnp.bfloat16)

    @pl.when(turn == 1)
    def give_values():
        kv_ref[...] = dv_ref[...]


def attention_backward(queries, keys, blended, grads, totals, limit, q_at, k_at, v_at, causal):
    rows, key_rows = (queries.shape[0], keys.shape[0])
    pairs = D // PAIR
    in_specs = [
        pl.BlockSpec((rows, PAIR), lambda p, t, _: (0, q_at * pairs + p)),
        pl.BlockSpec((key_rows, PAIR), lambda p, t, _: (0, k_at * pairs + p)),
        pl.BlockSpec((key_rows, PAIR), lambda p, t, _: (0, v_at * pairs + p)),
        pl.BlockSpec((rows, PAIR), lambda p, t, _: (0, p)),
        pl.BlockSpec((rows, PAIR), lambda p, t, _: (0, p)),
        pl.BlockSpec((None, 8, rows), lambda p, t, _: (p, 0, 0)),
    ]
    turned = [
        pltpu.VMEM((PAIR, rows), jnp.float32),
        pltpu.VMEM((PAIR, key_rows), jnp.bfloat16),
        pltpu.VMEM((8, rows), jnp.float32),
    ]
    kept = pltpu.VMEM((key_rows, PAIR), jnp.bfloat16)
    if causal:
        kernel, turns, scratch = (self_back, 3, [kept, kept] + turned)
        out_specs = [pl.BlockSpec((rows, PAIR), lambda p, t, _: (0, t * pairs + p))]
        out_shape = [jax.ShapeDtypeStruct((rows, 3 * D), jnp.bfloat16)]
    else:
        kernel, turns, scratch = (cross_back, 2, [kept] + turned)
        out_specs = [
            pl.BlockSpec((rows, PAIR), lambda p, t, _: (0, p)),
            pl.BlockSpec((key_rows, PAIR), lambda p, t, _: (0, t * pairs + p)),
        ]
        out_shape = [
            jax.ShapeDtypeStruct((rows, D), jnp.bfloat16),
            jax.ShapeDtypeStruct((key_rows, 2 * D), jnp.bfloat16),
        ]
    pixels = rows * key_rows * HEADS * (0.625 if causal else 1.0)
    return pl.pallas_call(
        kernel,
        grid_spec=pltpu.PrefetchScalarGridSpec(
            num_scalar_prefetch=1,
            grid=(pairs, turns),
            in_specs=in_specs,
            out_specs=out_specs,
            scratch_shapes=scratch,
        ),
        out_shape=out_shape,
        cost_estimate=pl.CostEstimate(
            flops=int(pixels * 1280 * 2), bytes_accessed=rows * D * 16, transcendentals=int(pixels)
        ),
    )(limit, queries, keys, keys, blended, grads, totals)


CHUNK = 8
HALF = TILE // 2
SIDE = 2 * TILE


def block_scale(squares):
    column = squares.sum(axis=0, keepdims=True)
    low = lane_half(column, 0).sum(axis=1, keepdims=True)
    high = lane_half(column, 1).sum(axis=1, keepdims=True)
    lanes = lax.broadcasted_iota(jnp.int32, column.shape, 1)
    mean = jnp.where(lanes < TILE, low, high) * (1.0 / (TILE * TILE))
    return lax.rsqrt(mean + stat_eps)


def swapped(values):
    return pltpu.roll(values, TILE, 1)


def mixed(low, high):
    lanes = lax.broadcasted_iota(jnp.int32, low.shape, 1)
    return jnp.where(lanes < TILE, low, high)


def shampoo_kernel(
    decay_ref, order_ref, g_ref, ls_ref, rs_ref, lr_ref, rr_ref,
    gout_ref, up_ref, ln_ref, rn_ref, lp_ref, rp_ref, lq_ref, rq_ref, n_ref, u_ref,
):
    decay = decay_ref[0]
    fresh = (1.0 - decay) * (1.0 / TILE)
    blocks = ls_ref.shape[0]
    order = order_ref[...]
    for chunk in range(0, blocks, CHUNK):
        count = min(CHUNK, blocks - chunk)
        here = slice(chunk, chunk + count)
        for piece in range(HALF):
            lanes = slice(piece * SIDE, (piece + 1) * SIDE)
            spread = pl.ds(piece, count, stride=HALF)
            lp_ref[spread, :] = lr_ref[here, lanes]
            rp_ref[spread, :] = rr_ref[here, lanes]
        for pair in range(count // 2):
            lanes = slice((chunk + 2 * pair) * TILE, (chunk + 2 * pair + 2) * TILE)
            first = slice(2 * pair * HALF, (2 * pair + 1) * HALF)
            second = slice((2 * pair + 1) * HALF, (2 * pair + 2) * HALF)
            at = pair * TILE
            raw = g_ref[:, lanes].astype(jnp.float32)
            gout_ref[:, lanes] = raw
            scaled = raw * block_scale(raw * raw)
            n_ref[at : at + TILE, :] = scaled
            scaled = scaled.astype(jnp.bfloat16)
            evens = n_ref[pl.ds(at, HALF, stride=2), :].astype(jnp.bfloat16)
            odds = n_ref[pl.ds(at + 1, HALF, stride=2), :].astype(jnp.bfloat16)
            sorted_cols = matmul(scaled, order).astype(jnp.bfloat16)
            diagonal = jnp.concatenate([lane_half(scaled, 0), lane_half(scaled, 1)], 0)
            outer = matmul(jnp.concatenate([evens, odds], 0), diagonal, NT)
            top, bottom = (outer[:HALF], outer[HALF:])
            lq_ref[first, :] = mixed(top, swapped(bottom))
            lq_ref[second, :] = mixed(swapped(top), bottom)
            gram = matmul(sorted_cols, scaled, (((0,), (0,)), ((), ())))
            rq_ref[first, :] = mixed(gram[:HALF], swapped(gram[HALF : 2 * HALF]))
            rq_ref[second, :] = mixed(swapped(gram[2 * HALF : 3 * HALF]), gram[3 * HALF :])
            left_a, left_b = (lp_ref[first, :], lp_ref[second, :])
            left = jnp.concatenate(
                [mixed(left_a, swapped(left_b)), mixed(swapped(left_a), left_b)], 0
            ).astype(jnp.bfloat16)
            wide = jnp.concatenate([lane_half(sorted_cols, 0), lane_half(sorted_cols, 1)], 0)
            shaped = matmul(left, wide).astype(jnp.bfloat16)
            right_a, right_b = (rp_ref[first, :], rp_ref[second, :])
            right = jnp.concatenate(
                [
                    lane_half(right_a, 0),
                    lane_half(swapped(right_a), 0),
                    lane_half(swapped(right_b), 1),
                    lane_half(right_b, 1),
                ],
                0,
            ).astype(jnp.bfloat16)
            shaped = matmul(shaped, right)
            direction = shaped * block_scale(shaped * shaped)
            u_ref[pl.ds(at, HALF, stride=2), :] = direction[:HALF]
            u_ref[pl.ds(at + 1, HALF, stride=2), :] = direction[HALF:]
            up_ref[:, lanes] = u_ref[at : at + TILE, :]
        for piece in range(HALF):
            lanes = slice(piece * SIDE, (piece + 1) * SIDE)
            spread = pl.ds(piece, count, stride=HALF)
            ln_ref[here, lanes] = decay * ls_ref[here, lanes] + fresh * lq_ref[spread, :]
            rn_ref[here, lanes] = decay * rs_ref[here, lanes] + fresh * rq_ref[spread, :]


def precondition(gradient, left_stat, right_stat, left_root, right_root, decay_rate, slots):
    stat_shape = left_stat.shape
    row_blocks, blocks = (stat_shape[-3], stat_shape[-2])
    steps = slots * row_blocks
    cols = blocks * TILE
    flat = (steps, blocks, TILE * TILE)
    source = lax.broadcasted_iota(jnp.int32, (SIDE, SIDE), 1)
    within = source % TILE
    source = source - within + jnp.where(within < HALF, 2 * within, 2 * within - TILE + 1)
    order = (lax.broadcasted_iota(jnp.int32, (SIDE, SIDE), 0) == source).astype(jnp.bfloat16)
    stat_spec = pl.BlockSpec((None, blocks, TILE * TILE), lambda s, _: (s, 0, 0))
    out_spec = pl.BlockSpec((None, TILE, cols), lambda s, _: (s, 0, 0))
    held = pltpu.VMEM((CHUNK * HALF, SIDE), jnp.float32)
    grads, update, left_new, right_new = pl.pallas_call(
        shampoo_kernel,
        grid_spec=pltpu.PrefetchScalarGridSpec(
            num_scalar_prefetch=1,
            grid=(steps,),
            in_specs=[
                pl.BlockSpec((SIDE, SIDE), lambda s, _: (0, 0)),
                pl.BlockSpec((TILE, cols), lambda s, _: (s % row_blocks, s // row_blocks)),
                stat_spec, stat_spec, stat_spec, stat_spec,
            ],
            out_specs=[out_spec, out_spec, stat_spec, stat_spec],
            scratch_shapes=[held] * 6,
        ),
        out_shape=(
            jax.ShapeDtypeStruct((steps, TILE, cols), jnp.float32),
            jax.ShapeDtypeStruct((steps, TILE, cols), jnp.float32),
            jax.ShapeDtypeStruct(flat, jnp.float32),
            jax.ShapeDtypeStruct(flat, jnp.float32),
        ),
        cost_estimate=pl.CostEstimate(
            flops=steps * blocks * 2000000, bytes_accessed=steps * blocks * 4096 * 34, transcendentals=0
        ),
    )(
        decay_rate.reshape(1),
        order,
        gradient,
        left_stat.reshape(flat),
        right_stat.reshape(flat),
        left_root.reshape(flat),
        right_root.reshape(flat),
    )
    full = stat_shape[:-3] + (row_blocks * TILE, cols)
    return (
        grads.reshape(full),
        update.reshape(full),
        left_new.reshape(stat_shape),
        right_new.reshape(stat_shape),
    )


def body(
    home_tokens,
    home_encoder,
    out_grad,
    lengths,
    enc_lengths,
    seq_order,
    attn_master,
    ffin_master,
    ffout_master,
    gain_master,
    decays,
    attn_left,
    attn_right,
    attn_left_root,
    attn_right_root,
    ffin_left,
    ffin_right,
    ffin_left_root,
    ffin_right_root,
    ffout_left,
    ffout_right,
    ffout_left_root,
    ffout_right_root,
    gain_stats,
):
    rows, enc_rows = (SEQ_LEN, ENC_LEN)
    order_row = seq_order[0]
    dealt_tokens, dealt_encoder = (
        lax.all_to_all(home_tokens[0][order_row], "fsdp", split_axis=0, concat_axis=1, tiled=True),
        lax.all_to_all(home_encoder[0][order_row], "fsdp", split_axis=0, concat_axis=1, tiled=True),
    )
    my_sequence = lax.dynamic_slice_in_dim(order_row, lax.axis_index("fsdp"), 1)
    dec_limit = lookup(lengths[0], my_sequence)
    enc_limit = lookup(enc_lengths[0], my_sequence)
    tokens = dealt_tokens.reshape(rows, D).astype(jnp.float32)
    encoder = dealt_encoder.reshape(enc_rows, D)
    positions = jnp.arange(SEQ_LEN, dtype=jnp.int32)
    valid_rows = (positions < dec_limit[0]).astype(jnp.float32)[:, None]

    def low(*matrices):
        return jnp.concatenate([matrix.astype(jnp.bfloat16) for matrix in matrices], -1)

    def gather(stack):
        return lax.all_gather(stack, "fsdp", axis=0, tiled=True)

    def scatter(grad):
        return lax.psum_scatter(grad.astype(jnp.bfloat16), "fsdp", scatter_dimension=0, tiled=True)

    gain_all = gather(gain_master.astype(jnp.bfloat16).T).T.astype(jnp.float32)
    self_in = gather(low(attn_master[0], attn_master[1], attn_master[2]))
    self_out = gather(low(attn_master[3]))
    cross_all = gather(low(attn_master[4], attn_master[5], attn_master[6]))
    cross_out = gather(low(attn_master[7]))
    feed_in = gather(low(ffin_master[0], ffin_master[1]))
    feed_out = gather(low(ffout_master))
    hidden_units = feed_out.shape[1]

    normed_one = rms_scale(tokens, gain_all[0]).astype(jnp.bfloat16)
    self_qkv = matmul(normed_one, self_in).astype(jnp.bfloat16)
    self_att, self_total = attention_forward(self_qkv, self_qkv, dec_limit, 0, 1, 2, True)
    hidden_one = tokens + matmul(self_att, self_out)
    normed_two = rms_scale(hidden_one, gain_all[1]).astype(jnp.bfloat16)
    cross_query = matmul(normed_two, cross_all[:, :D]).astype(jnp.bfloat16)
    cross_kv = matmul(encoder, cross_all[:, D:]).astype(jnp.bfloat16)
    cross_att, cross_total = attention_forward(cross_query, cross_kv, enc_limit, 0, 0, 1, False)
    hidden_two = hidden_one + matmul(cross_att, cross_out)
    normed_three = rms_scale(hidden_two, gain_all[2]).astype(jnp.bfloat16)
    gate_up = matmul(normed_three, feed_in)
    gate_part, up_part = (gate_up[:, :hidden_units], gate_up[:, hidden_units:])
    activated = gated_unit(gate_part, up_part).astype(jnp.bfloat16)
    result = hidden_two + matmul(activated, feed_out, NT)
    out_tokens = (result * valid_rows).astype(jnp.bfloat16).reshape(1, 1, SEQ_LEN, D)

    cols = (((0,), (0,)), ((), ()))
    grad_result = out_grad[0, 0].astype(jnp.float32) * valid_rows
    grad_branch = grad_result.astype(jnp.bfloat16)
    grad_activated = matmul(grad_branch, feed_out)
    unused, gate_pull = jax.vjp(gated_unit, gate_part, up_part)
    grad_gate, grad_up = gate_pull(grad_activated)
    grad_gate_up = low(grad_gate, grad_up)
    grad_normed = matmul(grad_gate_up, feed_in, NT)
    feed_out_part = scatter(matmul(grad_branch, activated, cols))
    feed_in_part = scatter(matmul(normed_three, grad_gate_up, cols))
    unused, norm_pull = jax.vjp(rms_scale, hidden_two, gain_all[2])
    grad_hidden, grad_gain_three = norm_pull(grad_normed)
    grad_hidden_two = grad_result + grad_hidden

    grad_cross_z = grad_hidden_two.astype(jnp.bfloat16)
    grad_cross_att = matmul(grad_cross_z, cross_out, NT).astype(jnp.bfloat16)
    cross_out_part = scatter(matmul(cross_att, grad_cross_z, cols))
    grad_cross_query, grad_cross_kv = attention_backward(
        cross_query, cross_kv, cross_att, grad_cross_att, cross_total, enc_limit, 0, 0, 1, False
    )
    grad_normed_two = matmul(grad_cross_query, cross_all[:, :D], NT)
    grad_encoder = matmul(grad_cross_kv, cross_all[:, D:], NT)
    cross_query_part = scatter(matmul(normed_two, grad_cross_query, cols))
    cross_kv_part = scatter(matmul(encoder, grad_cross_kv, cols))
    unused, norm_pull = jax.vjp(rms_scale, hidden_one, gain_all[1])
    grad_hidden, grad_gain_two = norm_pull(grad_normed_two)
    grad_hidden_one = grad_hidden_two + grad_hidden

    grad_self_z = grad_hidden_one.astype(jnp.bfloat16)
    grad_self_att = matmul(grad_self_z, self_out, NT).astype(jnp.bfloat16)
    self_out_part = scatter(matmul(self_att, grad_self_z, cols))
    (grad_self_qkv,) = attention_backward(
        self_qkv, self_qkv, self_att, grad_self_att, self_total, dec_limit, 0, 1, 2, True
    )
    self_in_part = scatter(matmul(normed_one, grad_self_qkv, cols))
    grad_normed_one = matmul(grad_self_qkv, self_in, NT)
    unused, norm_pull = jax.vjp(rms_scale, tokens, gain_all[0])
    grad_hidden, grad_gain_one = norm_pull(grad_normed_one)
    grad_tokens = grad_hidden_one + grad_hidden
    gain_part = scatter(jnp.stack([grad_gain_one, grad_gain_two, grad_gain_three], 1)).T

    back_tokens, back_encoder = (
        lax.all_to_all(
            grad_tokens.astype(jnp.bfloat16).reshape(1, SEQ_LEN, D),
            "fsdp",
            split_axis=1,
            concat_axis=0,
            tiled=True,
        ),
        lax.all_to_all(
            grad_encoder.astype(jnp.bfloat16).reshape(1, ENC_LEN, D),
            "fsdp",
            split_axis=1,
            concat_axis=0,
            tiled=True,
        ),
    )
    slot_ids = jnp.arange(order_row.shape[0], dtype=jnp.int32)
    inverse = jnp.sum(
        jnp.where(order_row[None, :] == slot_ids[:, None], slot_ids[None, :], 0), axis=1
    )
    token_grad = back_tokens[inverse][None]
    encoder_grad = back_encoder[inverse][None]

    def total(part):
        return lax.psum(part, "rep")

    attn_sum = total(
        jnp.concatenate(
            [self_in_part, self_out_part, cross_query_part, cross_kv_part, cross_out_part], 1
        )
    )
    feed_in_sum = total(feed_in_part)
    feed_out_sum = total(feed_out_part)
    gain_grad = total(gain_part).astype(jnp.float32)
    attn_grad, attn_update, attn_left_new, attn_right_new = precondition(
        attn_sum, attn_left, attn_right, attn_left_root, attn_right_root, decays[0], 8
    )
    ffin_grad, ffin_update, ffin_left_new, ffin_right_new = precondition(
        feed_in_sum, ffin_left, ffin_right, ffin_left_root, ffin_right_root, decays[1], 2
    )
    ffout_grad, ffout_update, ffout_left_new, ffout_right_new = precondition(
        feed_out_sum, ffout_left, ffout_right, ffout_left_root, ffout_right_root, decays[2], 1
    )
    gain_update, gain_stats_new = update_gains(gain_grad, gain_stats, decays[3])
    return (
        out_tokens,
        token_grad,
        encoder_grad,
        attn_grad,
        ffin_grad,
        ffout_grad,
        gain_grad,
        attn_update,
        ffin_update,
        ffout_update,
        gain_update,
        attn_left_new,
        attn_right_new,
        ffin_left_new,
        ffin_right_new,
        ffout_left_new,
        ffout_right_new,
        gain_stats_new,
    )


def solution(mesh):
    in_specs = (
        P("rep", None, "fsdp", None),
        P("rep", None, "fsdp", None),
        P("rep", "fsdp", None, None),
        P("rep", None),
        P("rep", None),
        P("rep", None),
        P(None, "fsdp", None),
        P(None, "fsdp", None),
        P("fsdp", None),
        P(None, "fsdp"),
        P(),
        P(None, "fsdp", None, None),
        P(None, "fsdp", None, None),
        P(None, "fsdp", None, None),
        P(None, "fsdp", None, None),
        P(None, "fsdp", None, None),
        P(None, "fsdp", None, None),
        P(None, "fsdp", None, None),
        P(None, "fsdp", None, None),
        P("fsdp", None, None),
        P("fsdp", None, None),
        P("fsdp", None, None),
        P("fsdp", None, None),
        P(None, "fsdp"),
    )
    out_specs = (
        P("rep", "fsdp", None, None),
        P("rep", None, "fsdp", None),
        P("rep", None, "fsdp", None),
        P(None, "fsdp", None),
        P(None, "fsdp", None),
        P("fsdp", None),
        P(None, "fsdp"),
        P(None, "fsdp", None),
        P(None, "fsdp", None),
        P("fsdp", None),
        P(None, "fsdp"),
        P(None, "fsdp", None, None),
        P(None, "fsdp", None, None),
        P(None, "fsdp", None, None),
        P(None, "fsdp", None, None),
        P("fsdp", None, None),
        P("fsdp", None, None),
        P(None, "fsdp"),
    )
    return jax.shard_map(body, mesh=mesh, in_specs=in_specs, out_specs=out_specs, check_vma=False)
```

time: 1760 us -> 1310 us (0.74)
  matrix products: 682 us -> 220 us
  waiting for transfers between devices: 163 us -> 551 us
  local copies, waits for them, and re-layouts: 449 us -> 98.8 us
  Pallas kernels: 0 us -> 253 us
  other arithmetic: 266 us -> 46 us
  blocking collectives: 137 us -> 84.3 us
    dot_general x61 -> x21, matrix products: 682 us -> 220 us  [matmul(): lax.dot_general(left_side, right_side, dims, preferred_element_type=jnp.f...]
    reduce_scatter x1 -> x7, waiting for transfers between devices: 63.6 us -> 335 us  [scatter(): lax.psum_scatter(grad.astype(jnp.bfloat16), 'fsdp', scatter_dimension=0,...]
    pallas_call x0 -> x7, Pallas kernels: none -> 253 us  [the longest x2 115 us: attention_backward(): pl.pallas_call(kernel, grid_spec=pltpu.PrefetchScalarGridSpec(num_scalar_...]
    all_gather x6, waiting for transfers between devices: 30.8 us -> 171 us  [gather(): return lax.all_gather(stack, 'fsdp', axis=0, tiled=True)]
    unnamed x189 -> x103, local copies, waits for them, and re-layouts: 190 us -> 74.4 us
    reshape x22 -> x2, local copies, waits for them, and re-layouts: 117 us -> 9.14 us  [the longest x1 7.52 us: body(): grad_tokens.astype(jnp.bfloat16).reshape(1, SEQ_LEN, D)]
    convert_element_type x14 -> x5, other arithmetic: 99.1 us -> 2.79 us  [the longest x1 0.93 us: low(): matrix.astype(jnp.bfloat16)]
    mul x10 -> x0, local copies, waits for them, and re-layouts: 72.5 us -> none  [the longest x3 27.6 us: precondition(): tile_grid * lax.rsqrt(jnp.mean(tile_grid * tile_grid, axis=(-2, -1), keep...]
  transfers between devices with their start and end apart: 17 -> 19, of which waited for: 5 -> 11; matrix products, arithmetic and copies ran while one was open for 57% -> 20% of each run, Pallas kernels for 0% -> 4%
where the time goes in v1:
time: 1310 us; the launch traced here: 1300 us
  waiting for transfers between devices  551 us (42%)
  Pallas kernels  253 us (19%)
  matrix products  220 us (17%)
  local copies, waits for them, and re-layouts  98.8 us (8%)
  blocking collectives  84.3 us (6%)
  other arithmetic  46 us (4%)
  starting transfers between devices  30.8 us (2%)
  between operations  15.6 us (1%)
    reduce_scatter x7, waiting for transfers between devices, scatter(): lax.psum_scatter(grad.astype(jnp.bfloat16), 'fsdp', scatter_dimension=0,...  335 us
    dot_general x21, matrix products, matmul(): lax.dot_general(left_side, right_side, dims, preferred_element_type=jnp.f...  220 us
    all_gather x6, waiting for transfers between devices, gather(): return lax.all_gather(stack, 'fsdp', axis=0, tiled=True)  171 us
    pallas_call x2, Pallas kernels, attention_backward(): pl.pallas_call(kernel, grid_spec=pltpu.PrefetchScalarGridSpec(num_scalar_...  115 us
    pallas_call x3, Pallas kernels, precondition(): pl.pallas_call(shampoo_kernel, grid_spec=pltpu.PrefetchScalarGridSpec(num...  80.4 us
    unnamed x103, local copies, waits for them, and re-layouts  74.4 us
    all_gather x1, blocking collectives, gather(): return lax.all_gather(stack, 'fsdp', axis=0, tiled=True)  74 us
    pallas_call x2, Pallas kernels, attention_forward(): pl.pallas_call(functools.partial(forward_kernel, causal), grid_spec=grid_...  57.7 us
  transfers between devices with their start and end apart: 19, of which 11 were waited for; matrix products, arithmetic and copies ran while one was open for 20% of the time, Pallas kernels for 4%

profile of v1, /device:TPU:0, one launch (start us, length us, event | category | flops | bytes accessed | tf_op | source)
XLA Modules:
  0.0 1299.2 jit_solution(13538564481436474299)
XLA Ops:
  28.4 74.0 %all_gather.21 = bf16[1024,3]{0,1:T(4,128)(2,1)S(1)} all-gather(bf16[128,3]{0,1:T(4,128)(2,1)S(1)} %convert_bitcast_fusion.1), channel_id=1, replica_groups=mesh['rep'=4,'fsdp'=8] {'fsdp'}, dimensions={0}, use_global_device_ids=true | all-gather | bytes 6912 | tf_op jit(solution)/shard_map/all_gather | solution.py:458
  121.9 16.4 %all-to-all-start.1 = ((bf16[8,64,1024]{2,1,0:T(8,128)(2,1)}), bf16[8,64,1024]{2,1,0:T(8,128)(2,1)S(1)}, u32[]{:S(2)}, u32[]{:S(2)}) async-start(bf16[8,64,1024]{2,1,0:T(8,128)(2,1)} %gather_fusion.1), calls=%async_computation.1 | async-start | bytes 2097152 | tf_op jit(solution)/shard_map/all_to_all | solution.py:444
  154.5 30.0 %shard_map.367 = (bf16[1024,1024]{1,0:T(8,128)(2,1)}, f32[8,8,1024]{2,1,0:T(8,128)}) custom-call(s32[1]{0:T(128)} %bitcast.5.limit_ref, bf16[1024,3072]{1,0:T(8,128)(2,1)} %convolution_convert_fusion.3.q_ref.k_ref.v_ref, bf16[1024,3072]{1,0:T(8,128)(2,1)} %convolution_convert_fusion.3.q_ref.k_ref.v_ref, ...), custom_call_target="tpu_custom_call" | custom-call | flops 10737418240 | bytes 8388608 | tf_op jit(solution)/shard_map/pallas_call | solution.py:170
  192.6 40.7 %all-gather.11.cloned.1.call-done = bf16[1024,3072]{1,0:T(8,128)(2,1)} async-done(((bf16[128,3072]{1,0:T(8,128)(2,1)}), bf16[1024,3072]{1,0:T(8,128)(2,1)}) %all-gather.11.cloned.1.call-update) | async-done | bytes 6291472 | tf_op jit(solution)/shard_map/all_gather | solution.py:458
  244.9 27.7 %shard_map.368 = (bf16[1024,1024]{1,0:T(8,128)(2,1)}, f32[8,8,1024]{2,1,0:T(8,128)}) custom-call(s32[1]{0:T(128)} %bitcast.14.limit_ref, bf16[1024,1024]{1,0:T(8,128)(2,1)} %convolution_convert_fusion.8.q_ref, bf16[512,2048]{1,0:T(8,128)(2,1)} %fusion.16.k_ref.v_ref, bf16[512,2048]{1,0:T(8,128)(2,1)} %fusion.16.k_ref.v_ref), custom_call_target="tpu_custom_call" | custom-call | flops 8589934592 | bytes 8388608 | tf_op jit(solution)/shard_map/pallas_call | solution.py:170
  281.8 91.0 %all-gather.13.cloned.1.call-done = bf16[1024,5632]{1,0:T(8,128)(2,1)} async-done(((bf16[128,5632]{1,0:T(8,128)(2,1)}), bf16[1024,5632]{1,0:T(8,128)(2,1)}) %all-gather.13.cloned.1.call-update) | async-done | bytes 11534352 | tf_op jit(solution)/shard_map/all_gather | solution.py:458
  372.8 21.5 %fusion.73 = f32[1024,5632]{1,0:T(8,128)} fusion(bf16[1024,5632]{1,0:T(8,128)(2,1)} %all-gather.13.cloned.1.call-done, f32[1024,1024]{0,1:T(8,128)} %get-tuple-element.178, f32[1024]{0:T(1024)S(1)} %bitcast.161, f32[1024]{0:T(1024)S(1)} %fusion.65), kind=kOutput, calls=%fused_computation.141 | convolution fusion | flops 11814305792 | bytes 38805504 | tf_op jit(solution)/shard_map/dot_general | solution.py:61
  394.3 39.2 %all-gather.15.cloned.1.call-done = bf16[1024,2816]{1,0:T(8,128)(2,1)} async-done(((bf16[128,2816]{1,0:T(8,128)(2,1)}), bf16[1024,2816]{1,0:T(8,128)(2,1)}) %all-gather.15.cloned.1.call-update) | async-done | bytes 5767184 | tf_op jit(solution)/shard_map/all_gather | solution.py:458
  433.5 23.8 %fusion.3 = (bf16[1024,2816]{1,0:T(8,128)(2,1)}, bf16[1024,2816]{1,0:T(8,128)(2,1)}, bf16[1024,2816]{1,0:T(8,128)(2,1)}) fusion(f32[1024,5632]{1,0:T(8,128)} %fusion.73, bf16[1024,2816]{1,0:T(8,128)(2,1)} %all-gather.15.cloned.1.call-done, bf16[1,1,1024,1024]{2,3,1,0:T(8,128)(2,1)S(1)} %copy-done.5, f32[1024]{0:T(1024)S(1)} %fusion.63), kind=kOutput, calls=%fused_computation.11 | convolution fusion | flops 5995233280 | bytes 48238592 | tf_op jit(solution)/shard_map/dot_general | solution.py:61
  457.3 21.5 %multiply_reduce_fusion = (bf16[1024]{0:T(1024)(128)(2,1)}, f32[1024]{0:T(1024)S(1)}, f32[1024,1024]{0,1:T(8,128)}) fusion(f32[1024,1024]{0,1:T(8,128)} %get-tuple-element.178, f32[1024]{0:T(1024)S(1)} %fusion.65, f32[1024]{0:T(1024)S(1)} %bitcast.162, bf16[1024,5632]{1,0:T(8,128)(2,1)} %all-gather.13.cloned.1.call-done, ...), kind=kOutput, calls=%fused_computation.32 | convolution fusion | flops 11840518144 | bytes 31471616 | tf_op jit(solution)/shard_map/dot_general | solution.py:61
  486.2 48.8 %shard_map.369 = (bf16[1024,1024]{1,0:T(8,128)(2,1)}, bf16[512,2048]{1,0:T(8,128)(2,1)}) custom-call(s32[1]{0:T(128)} %bitcast.14.limit_ref, bf16[1024,1024]{1,0:T(8,128)(2,1)} %convolution_convert_fusion.8.q_ref, bf16[512,2048]{1,0:T(8,128)(2,1)} %fusion.16.k_ref.v_ref, bf16[512,2048]{1,0:T(8,128)(2,1)} %fusion.16.k_ref.v_ref, ...), custom_call_target="tpu_custom_call" | custom-call | flops 21474836480 | bytes 16777216 | tf_op jit(solution)/shard_map/pallas_call | solution.py:257
  546.8 65.7 %shard_map.370 = bf16[1024,3072]{1,0:T(8,128)(2,1)} custom-call(s32[1]{0:T(128)} %bitcast.5.limit_ref, bf16[1024,3072]{1,0:T(8,128)(2,1)} %convolution_convert_fusion.3.q_ref.k_ref.v_ref, bf16[1024,3072]{1,0:T(8,128)(2,1)} %convolution_convert_fusion.3.q_ref.k_ref.v_ref, bf16[1024,3072]{1,0:T(8,128)(2,1)} %convolution_convert_fusion.3.q_ref.k_ref.v_ref, ...), custom_call_target="tpu_custom_call" | custom-call | flops 26843545600 | bytes 16777216 | tf_op jit(solution)/shard_map/pallas_call | solution.py:257
  661.8 20.1 %convolution_convert_fusion = bf16[1024,5632]{1,0:T(8,128)(2,1)} fusion(bf16[1024,2816]{1,0:T(8,128)(2,1)} %get-tuple-element.156, bf16[1024,2816]{1,0:T(8,128)(2,1)} %get-tuple-element.155, f32[1024,1024]{0,1:T(8,128)} %get-tuple-element.178, f32[1024]{0:T(1024)S(1)} %bitcast.164, f32[1024]{0:T(1024)S(1)} %fusion.65), kind=kOutput, calls=%fused_computation.17 | convolution fusion | flops 11843141632 | bytes 27271168 | tf_op jit(solution)/shard_map/dot_general | solution.py:61
  682.0 13.6 %multiply_reduce_fusion.2 = (bf16[1024]{0:T(1024)(128)(2,1)S(1)}, f32[1024]{0:T(1024)S(1)}, f32[1024,1024]{0,1:T(8,128)}) fusion(f32[1024,1024]{0,1:T(8,128)} %copy.163, f32[1024]{0:T(1024)S(1)} %copy-done.26, f32[1024]{0:T(1024)S(1)} %bitcast.171, bf16[1024,3072]{1,0:T(8,128)(2,1)} %shard_map.370, bf16[1024,3072]{1,0:T(8,128)(2,1)} %all-gather.9.cloned.1.call-done), kind=kOutput, calls=%fused_computation.34 | convolution fusion | flops 6448740352 | bytes 20985856 | tf_op jit(solution)/shard_map/dot_general | solution.py:61
  716.6 20.5 %reduce-scatter.13.cloned.1.call-done = bf16[128,1024]{1,0:T(8,128)(2,1)} async-done(((bf16[1024,1024]{1,0:T(8,128)(2,1)}), bf16[128,1024]{1,0:T(8,128)(2,1)}) %reduce-scatter.13.cloned.1.call-update) | async-done | bytes 262160 | tf_op jit(solution)/shard_map/reduce_scatter | solution.py:461
  738.0 43.9 %reduce-scatter.15.cloned.1.call-done = bf16[128,1024]{1,0:T(8,128)(2,1)} async-done(((bf16[1024,1024]{1,0:T(8,128)(2,1)}), bf16[128,1024]{1,0:T(8,128)(2,1)}) %reduce-scatter.15.cloned.1.call-update) | async-done | bytes 262160 | tf_op jit(solution)/shard_map/reduce_scatter | solution.py:461
  782.8 49.8 %reduce-scatter.17.cloned.1.call-done = bf16[128,2048]{1,0:T(8,128)(2,1)} async-done(((bf16[1024,2048]{1,0:T(8,128)(2,1)}), bf16[128,2048]{1,0:T(8,128)(2,1)}) %reduce-scatter.17.cloned.1.call-update) | async-done | bytes 524304 | tf_op jit(solution)/shard_map/reduce_scatter | solution.py:461
  833.7 36.3 %reduce-scatter.19.cloned.1.call-done = bf16[128,1024]{1,0:T(8,128)(2,1)} async-done(((bf16[1024,1024]{1,0:T(8,128)(2,1)}), bf16[128,1024]{1,0:T(8,128)(2,1)}) %reduce-scatter.19.cloned.1.call-update) | async-done | bytes 262160 | tf_op jit(solution)/shard_map/reduce_scatter | solution.py:461
  871.0 64.6 %reduce-scatter.23.cloned.1.call-done = bf16[128,2816]{1,0:T(8,128)(2,1)} async-done(((bf16[1024,2816]{1,0:T(8,128)(2,1)}), bf16[128,2816]{1,0:T(8,128)(2,1)}) %reduce-scatter.23.cloned.1.call-update) | async-done | bytes 720912 | tf_op jit(solution)/shard_map/reduce_scatter | solution.py:461
  935.6 120.0 %reduce-scatter.21.cloned.1.call-done = bf16[128,5632]{1,0:T(8,128)(2,1)} async-done(((bf16[1024,5632]{1,0:T(8,128)(2,1)}), bf16[128,5632]{1,0:T(8,128)(2,1)}) %reduce-scatter.21.cloned.1.call-update) | async-done | bytes 1441808 | tf_op jit(solution)/shard_map/reduce_scatter | solution.py:461
  1160.4 34.6 %all-reduce.3.cloned.1.call-done = (bf16[128,8192]{1,0:T(8,128)(2,1)}, bf16[128,5632]{1,0:T(8,128)(2,1)}, bf16[128,2816]{1,0:T(8,128)(2,1)}) async-done(((bf16[128,8192]{1,0:T(8,128)(2,1)}, bf16[128,5632]{1,0:T(8,128)(2,1)}, bf16[128,2816]{1,0:T(8,128)(2,1)}), (bf16[128,8192]{1,0:T(8,128)(2,1)}, bf16[128,5632]{1,0:T(8,128)(2,1)}, bf16[128,2816]{1,0:T(8,128)(2,1)})) %all-reduce.3.cloned.1.call-update) | async-done | bytes 4259856 | tf_op jit(solution)/shard_map/psum | solution.py:553
  1194.9 26.4 %shard_map.372 = (f32[4,64,2816]{2,1,0:T(8,128)}, f32[4,64,2816]{2,1,0:T(8,128)}, f32[4,44,4096]{2,1,0:T(8,128)}, f32[4,44,4096]{2,1,0:T(8,128)}) custom-call(f32[1]{0:T(128)} %get-tuple-element.172.decay_ref, bf16[128,128]{1,0:T(8,128)(2,1)} %fusion.59.order_ref, bf16[128,5632]{1,0:T(8,128)(2,1)} %get-tuple-element.151.g_ref, f32[4,44,4096]{2,1,0:T(8,128)} %bitcast.142, ...), custom_call_target="tpu_custom_call" | custom-call | flops 352000000 | bytes 24510464 | tf_op jit(solution)/shard_map/pallas_call | solution.py:374
  1231.0 15.6 %shard_map.373 = (f32[2,64,2816]{2,1,0:T(8,128)}, f32[2,64,2816]{2,1,0:T(8,128)}, f32[2,44,4096]{2,1,0:T(8,128)}, f32[2,44,4096]{2,1,0:T(8,128)}) custom-call(f32[1]{0:T(128)} %get-tuple-element.174.decay_ref, bf16[128,128]{1,0:T(8,128)(2,1)} %fusion.59.order_ref, bf16[128,2816]{1,0:T(8,128)(2,1)} %get-tuple-element.152.g_ref, f32[2,44,4096]{2,1,0:T(8,128)} %copy.147.ls_ref, ...), custom_call_target="tpu_custom_call" | custom-call | flops 176000000 | bytes 12255232 | tf_op jit(solution)/shard_map/pallas_call | solution.py:374
  1253.9 38.3 %shard_map.371 = (f32[16,64,1024]{2,1,0:T(8,128)}, f32[16,64,1024]{2,1,0:T(8,128)}, f32[16,16,4096]{2,1,0:T(8,128)}, f32[16,16,4096]{2,1,0:T(8,128)}) custom-call(f32[1]{0:T(128)} %get-tuple-element.173.decay_ref, bf16[128,128]{1,0:T(8,128)(2,1)} %fusion.59.order_ref, bf16[128,8192]{1,0:T(8,128)(2,1)} %get-tuple-element.150.g_ref, ...), custom_call_target="tpu_custom_call" | custom-call | flops 512000000 | bytes 35651584 | tf_op jit(solution)/shard_map/pallas_call | solution.py:374
  (217 shorter events, 299.6 us)
Async XLA Ops:
  7.2 135.2 %all-gather.9.cloned.1.call-start = ((), (), s32[]{:S(2)}) async-start(), calls=%async_computation.12 | async-start | bytes 7077888 | tf_op jit(solution)/shard_map/all_gather | solution.py:458
  11.9 172.7 %all-gather.17.cloned.1.call-start = ((), (), s32[]{:S(2)}) async-start(), calls=%async_computation.23 | async-start | bytes 2359296 | tf_op jit(solution)/shard_map/all_gather | solution.py:458
  12.6 220.7 %all-gather.11.cloned.1.call-start = ((), (), s32[]{:S(2)}) async-start(), calls=%async_computation.13 | async-start | bytes 7077888 | tf_op jit(solution)/shard_map/all_gather | solution.py:458
  13.7 259.0 %all-gather.19.cloned.1.call-start = ((), (), s32[]{:S(2)}) async-start(), calls=%async_computation.24 | async-start | bytes 2359296 | tf_op jit(solution)/shard_map/all_gather | solution.py:458
  14.2 358.5 %all-gather.13.cloned.1.call-start = ((), (), s32[]{:S(2)}) async-start(), calls=%async_computation.14 | async-start | bytes 12976128 | tf_op jit(solution)/shard_map/all_gather | solution.py:458
  20.3 82.1 %copy-start.36 = (s32[1,8]{1,0:T(1,128)S(1)}, s32[1,8]{1,0:T(1,128)}, u32[]{:S(2)}) copy-start(s32[1,8]{1,0:T(1,128)} %param.27) | copy-start | bytes 100
  20.3 101.6 %all-to-all-start = ((bf16[8,128,1024]{2,1,0:T(8,128)(2,1)}), bf16[8,128,1024]{2,1,0:T(8,128)(2,1)S(1)}, u32[]{:S(2)}, u32[]{:S(2)}) async-start(bf16[8,128,1024]{2,1,0:T(8,128)(2,1)} %gather_fusion), calls=%async_computation | async-start | bytes 4194304 | tf_op jit(solution)/shard_map/all_to_all | solution.py:443
  26.8 406.7 %all-gather.15.cloned.1.call-start = ((), (), s32[]{:S(2)}) async-start(), calls=%async_computation.15 | async-start | bytes 6488064 | tf_op jit(solution)/shard_map/all_gather | solution.py:458
  121.9 70.8 %all-to-all-start.1 = ((bf16[8,64,1024]{2,1,0:T(8,128)(2,1)}), bf16[8,64,1024]{2,1,0:T(8,128)(2,1)S(1)}, u32[]{:S(2)}, u32[]{:S(2)}) async-start(bf16[8,64,1024]{2,1,0:T(8,128)(2,1)} %gather_fusion.1), calls=%async_computation.1 | async-start | bytes 2097152 | tf_op jit(solution)/shard_map/all_to_all | solution.py:444
  138.2 577.1 %reduce-scatter.11.cloned.1.call-start = ((), (), s32[]{:S(2)}) async-start(), calls=%async_computation.16 | async-start | bytes 7077888 | tf_op jit(solution)/shard_map/reduce_scatter | solution.py:461
  372.8 60.7 %copy-start.5 = (bf16[1,1,1024,1024]{2,3,1,0:T(8,128)(2,1)S(1)}, bf16[1,1,1024,1024]{2,3,1,0:T(8,128)(2,1)}, u32[]{:S(2)}) copy-start(bf16[1,1,1024,1024]{2,3,1,0:T(8,128)(2,1)} %copy.137) | copy-start | bytes 6291460
  546.8 65.7 %copy-start.26 = (f32[1024]{0:T(1024)S(1)}, f32[1024]{0:T(1024)}, u32[]{:S(2)}) copy-start(f32[1024]{0:T(1024)} %copy-done.25) | copy-start | bytes 12292
  546.8 65.7 %copy-start.28 = (f32[1,1024]{1,0:T(1,128)S(1)}, f32[1,1024]{1,0:T(1,128)}, u32[]{:S(2)}) copy-start(f32[1,1024]{1,0:T(1,128)} %copy-done.27) | copy-start | bytes 12292
  624.9 112.1 %reduce-scatter.13.cloned.1.call-start = ((), (), s32[]{:S(2)}) async-start(), calls=%async_computation.17 | async-start | bytes 2359296 | tf_op jit(solution)/shard_map/reduce_scatter | solution.py:461
  631.5 150.3 %reduce-scatter.15.cloned.1.call-start = ((), (), s32[]{:S(2)}) async-start(), calls=%async_computation.18 | async-start | bytes 2359296 | tf_op jit(solution)/shard_map/reduce_scatter | solution.py:461
  638.2 194.4 %reduce-scatter.17.cloned.1.call-start = ((), (), s32[]{:S(2)}) async-start(), calls=%async_computation.19 | async-start | bytes 4718592 | tf_op jit(solution)/shard_map/reduce_scatter | solution.py:461
  644.3 225.8 %reduce-scatter.19.cloned.1.call-start = ((), (), s32[]{:S(2)}) async-start(), calls=%async_computation.20 | async-start | bytes 2359296 | tf_op jit(solution)/shard_map/reduce_scatter | solution.py:461
  650.9 284.7 %reduce-scatter.23.cloned.1.call-start = ((), (), s32[]{:S(2)}) async-start(), calls=%async_computation.22 | async-start | bytes 6488064 | tf_op jit(solution)/shard_map/reduce_scatter | solution.py:461
  661.8 393.9 %reduce-scatter.21.cloned.1.call-start = ((), (), s32[]{:S(2)}) async-start(), calls=%async_computation.21 | async-start | bytes 12976128 | tf_op jit(solution)/shard_map/reduce_scatter | solution.py:461
  710.7 374.7 %all-to-all-start.3 = ((bf16[8,2,32768]{2,1,0:T(2,128)(2,1)}), bf16[8,2,32768]{2,1,0:T(2,128)(2,1)S(1)}, u32[]{:S(2)}, u32[]{:S(2)}) async-start(bf16[8,2,32768]{2,1,0:T(2,128)(2,1)} %reshape.342), calls=%async_computation.3 | async-start | bytes 2097152 | tf_op jit(solution)/shard_map/all_to_all | solution.py:537
  714.3 416.0 %reduce-scatter.25.cloned.1.call-start = ((), (), s32[]{:S(2)}) async-start(), calls=%async_computation.25 | async-start | bytes 294912
  715.3 479.6 %all-reduce.3.cloned.1.call-start = ((), (), s32[]{:S(2)}) async-start(), calls=%async_computation.26 | async-start | bytes 8519680 | tf_op jit(solution)/shard_map/psum | solution.py:553
  871.0 184.6 %copy-start.9 = (bf16[128,8192]{1,0:T(8,128)(2,1)}, bf16[128,8192]{1,0:T(8,128)(2,1)S(1)}, u32[]{:S(2)}) copy-start(bf16[128,8192]{1,0:T(8,128)(2,1)S(1)} %constant_dynamic-update-slice_fusion) | copy-start | bytes 6291460
  1085.4 65.5 %all-to-all-start.2 = ((bf16[8,2,65536]{2,1,0:T(2,128)(2,1)}), bf16[8,2,65536]{2,1,0:T(2,128)(2,1)S(1)}, u32[]{:S(2)}, u32[]{:S(2)}) async-start(bf16[8,2,65536]{2,1,0:T(2,128)(2,1)} %reshape.340), calls=%async_computation.2 | async-start | bytes 4194304 | tf_op jit(solution)/shard_map/all_to_all | solution.py:530
  (33 other events, 378.3 us)
Sparse Core Ops, SparseCore 0:
  12.0 111.9 all-gather.8
  126.2 37.8 all-gather.16
  166.4 66.9 all-gather.10
  235.4 27.7 all-gather.18
  265.3 107.4 all-gather.12
  374.8 58.5 all-gather.14
  625.0 68.3 reduce-scatter.10
  696.3 40.6 reduce-scatter.12
  739.9 41.9 reduce-scatter.14
  784.0 48.6 reduce-scatter.16
  835.5 34.4 reduce-scatter.18
  872.2 63.3 reduce-scatter.22
  937.9 117.6 reduce-scatter.20
  1058.3 29.2 reduce-scatter.24
  1091.8 103.1 all-reduce.2
